TPU v7x, 8 devices: a whole 2x2x1 slice. The times are simulated.
8 devices in a mesh: pairs: 1 (over z), rows: 8 (over y, x, core).
Axes of the slice: x: 2, y: 2, z: 1, core: 2. Of those that a mesh axis runs over, the one named last changes fastest.
Arguments:
- cost_src: float32 [2048, 2048], P(('pairs', 'rows'))
- cost_tgt: float32 [2048, 2048], P(('pairs', 'rows'))
- plan_init: float32 [2048, 2048], P(('pairs', 'rows'))
- mass_src: float32 [2048], P(('pairs', 'rows'))
- mass_tgt: float32 [2048], P('pairs')
- feat_src: float32 [2048, 256], P(('pairs', 'rows'))
- feat_tgt: float32 [2048, 256], P(('pairs', 'rows'))
- epsilon: float32 [], replicated
Outputs:
- output: float32 [2048, 2048], P(('pairs', 'rows'))
All inputs are finite; a program needn't handle non-finite values.
Results may differ from a plain program's by a relative error of at most 0.001.
Values are sent between devices in bfloat16 or wider.
A program may use at most 1 GiB of HBM per device.

v0:
```python
import jax
import jax.numpy as jnp
from jax import lax
from jax.sharding import PartitionSpec as P

ALPHA = 0.5
OUTER_STEPS = 2
SWEEPS = 10


def gibbs_kernel(cost_rows, epsilon):
    return jnp.exp(-(cost_rows - jnp.min(cost_rows, axis=1, keepdims=True)) / epsilon)


def scaled_plan(kernel, mass_rows, mass_tgt):
    def value_a14(sweep_index, scales):
        row_scale = mass_rows / jnp.sum(kernel * scales[1][None, :], axis=1)
        col_sum = lax.psum(jnp.sum(kernel * row_scale[:, None], axis=0), 'rows')
        return row_scale, mass_tgt / col_sum
    start_scales = (jnp.ones_like(mass_rows), jnp.ones_like(mass_tgt))
    row_scale, col_scale = lax.fori_loop(0, SWEEPS, value_a14, start_scales)
    return row_scale[:, None] * kernel * col_scale[None, :]


def solution(mesh):
    def local_fgw(cost_src, cost_tgt, plan_init, mass_src, mass_tgt, feat_src, feat_tgt, epsilon):
        src_half = cost_src.astype(jnp.bfloat16)
        tgt_half = cost_tgt.astype(jnp.bfloat16)
        feat_all = lax.all_gather(feat_tgt.astype(jnp.bfloat16), 'rows', tiled=True)
        cross_term = jnp.einsum('id,jd->ij', feat_src.astype(jnp.bfloat16), feat_all, preferred_element_type=jnp.float32)
        feat_cost = (-2.0 * ALPHA) * cross_term
        transport = plan_init
        for step_index in range(OUTER_STEPS):
            transport_all = lax.all_gather(transport.astype(jnp.bfloat16), 'rows', tiled=True)
            tgt_all = lax.all_gather(tgt_half, 'rows', tiled=True)
            prod_a = jnp.dot(src_half, transport_all, preferred_element_type=jnp.float32)
            prod_b = jnp.dot(prod_a.astype(jnp.bfloat16), tgt_all, preferred_element_type=jnp.float32)
            step_cost = feat_cost - (2.0 * (1.0 - ALPHA)) * prod_b
            transport = scaled_plan(gibbs_kernel(step_cost, epsilon), mass_src, mass_tgt)
        return transport

    row_spec = P(('pairs', 'rows'), None)
    vec_spec = P(('pairs', 'rows'))
    in_specs = (row_spec, row_spec, row_spec, vec_spec, P('pairs'), row_spec, row_spec, P())
    return jax.shard_map(local_fgw, mesh=mesh, in_specs=in_specs, out_specs=row_spec, check_vma=False)
```

profile of v0, /device:TPU:0, one launch (start us, length us, event | category | flops | bytes accessed | tf_op | source)
XLA Modules:
  0.0 707.1 jit_solution(16917003419787735615)
XLA Ops:
  8.2 2.9 convert_element_type.30
  13.1 16.4 %all-gather.5.cloned.1.call-done = bf16[2048,256]{1,0:T(8,128)(2,1)} async-done(((bf16[256,256]{1,0:T(8,128)(2,1)}), bf16[2048,256]{1,0:T(8,128)(2,1)}) %all-gather.5.cloned.1.call-update) | async-done | bytes 1048592 | tf_op jit(solution)/shard_map/all_gather | solution.py:29
  31.3 48.5 %all-gather.9.cloned.1.call-done = bf16[2048,2048]{1,0:T(8,128)(2,1)} async-done(((bf16[256,2048]{1,0:T(8,128)(2,1)}), bf16[2048,2048]{1,0:T(8,128)(2,1)}) %all-gather.9.cloned.1.call-update) | async-done | bytes 8388624 | tf_op jit(solution)/shard_map/all_gather | solution.py:35
  79.7 50.2 %all-gather.7.cloned.1.call-done = bf16[2048,2048]{1,0:T(8,128)(2,1)} async-done(((bf16[256,2048]{1,0:T(8,128)(2,1)}), bf16[2048,2048]{1,0:T(8,128)(2,1)}) %all-gather.7.cloned.1.call-update) | async-done | bytes 8388624 | tf_op jit(solution)/shard_map/all_gather | solution.py:34
  129.9 12.3 %fusion.5 = (f32[256]{0:T(256)S(1)}, f32[256,2048]{1,0:T(8,128)}) fusion(f32[256,2048]{1,0:T(8,128)S(1)} %convolution_multiply_fusion, bf16[2048,2048]{1,0:T(8,128)(2,1)} %all-gather.9.cloned.1.call-done, bf16[2048,2048]{1,0:T(8,128)(2,1)} %all-gather.7.cloned.1.call-done, f32[256,2048]{1,0:T(8,128)} %param.12), kind=kOutput, calls=%fused_computation.18 | convolution fusion | flops 4297064448 | bytes 23069696 | tf_op jit(solution)/shard_map/dot_general | solution.py:37
  142.2 2.0 divide_exponential_fusion.1
  144.8 240.3 %while.26 = (s32[]{:T(128)}, f32[256]{0:T(256)}, f32[2048]{0:T(1024)S(1)}, f32[256,2048]{1,0:T(8,128)S(1)}, f32[256]{0:T(256)S(1)}, /*index=5*/f32[2048]{0:T(1024)S(1)}, s32[]{:T(128)}, s32[]{:T(128)}) while((s32[]{:T(128)}, f32[256]{0:T(256)}, f32[2048]{0:T(1024)S(1)}, f32[256,2048]{1,0:T(8,128)S(1)}, f32[256]{0:T(256)S(1)}, ...), condition=%wide.region_5.0_spmd.clone, body=%wide.region_1.0_spmd.clone.sunk | while | flops 2101251 | bytes 4277371 | solution.py:21
  145.3 22.3 %psum.18 = f32[2048]{0:T(1024)S(1)} all-reduce(f32[2048]{0:T(1024)S(1)} %multiply_reduce_fusion.9), channel_id=1, replica_groups=mesh['pairs'=1,'rows'=8] {'rows'}, use_global_device_ids=true, to_apply=%region_4.0 | all-reduce | flops 2048 | bytes 16384 | tf_op jit(solution)/shard_map/while/body/eval_jaxpr/psum | solution.py:18
  168.1 24.1 %psum.18 = f32[2048]{0:T(1024)S(1)} all-reduce(f32[2048]{0:T(1024)S(1)} %multiply_reduce_fusion.9), channel_id=1, replica_groups=mesh['pairs'=1,'rows'=8] {'rows'}, use_global_device_ids=true, to_apply=%region_4.0 | all-reduce | flops 2048 | bytes 16384 | tf_op jit(solution)/shard_map/while/body/eval_jaxpr/psum | solution.py:18
  192.7 23.1 %psum.18 = f32[2048]{0:T(1024)S(1)} all-reduce(f32[2048]{0:T(1024)S(1)} %multiply_reduce_fusion.9), channel_id=1, replica_groups=mesh['pairs'=1,'rows'=8] {'rows'}, use_global_device_ids=true, to_apply=%region_4.0 | all-reduce | flops 2048 | bytes 16384 | tf_op jit(solution)/shard_map/while/body/eval_jaxpr/psum | solution.py:18
  216.3 24.1 %psum.18 = f32[2048]{0:T(1024)S(1)} all-reduce(f32[2048]{0:T(1024)S(1)} %multiply_reduce_fusion.9), channel_id=1, replica_groups=mesh['pairs'=1,'rows'=8] {'rows'}, use_global_device_ids=true, to_apply=%region_4.0 | all-reduce | flops 2048 | bytes 16384 | tf_op jit(solution)/shard_map/while/body/eval_jaxpr/psum | solution.py:18
  240.9 23.1 %psum.18 = f32[2048]{0:T(1024)S(1)} all-reduce(f32[2048]{0:T(1024)S(1)} %multiply_reduce_fusion.9), channel_id=1, replica_groups=mesh['pairs'=1,'rows'=8] {'rows'}, use_global_device_ids=true, to_apply=%region_4.0 | all-reduce | flops 2048 | bytes 16384 | tf_op jit(solution)/shard_map/while/body/eval_jaxpr/psum | solution.py:18
  264.6 24.1 %psum.18 = f32[2048]{0:T(1024)S(1)} all-reduce(f32[2048]{0:T(1024)S(1)} %multiply_reduce_fusion.9), channel_id=1, replica_groups=mesh['pairs'=1,'rows'=8] {'rows'}, use_global_device_ids=true, to_apply=%region_4.0 | all-reduce | flops 2048 | bytes 16384 | tf_op jit(solution)/shard_map/while/body/eval_jaxpr/psum | solution.py:18
  289.1 23.1 %psum.18 = f32[2048]{0:T(1024)S(1)} all-reduce(f32[2048]{0:T(1024)S(1)} %multiply_reduce_fusion.9), channel_id=1, replica_groups=mesh['pairs'=1,'rows'=8] {'rows'}, use_global_device_ids=true, to_apply=%region_4.0 | all-reduce | flops 2048 | bytes 16384 | tf_op jit(solution)/shard_map/while/body/eval_jaxpr/psum | solution.py:18
  312.8 24.1 %psum.18 = f32[2048]{0:T(1024)S(1)} all-reduce(f32[2048]{0:T(1024)S(1)} %multiply_reduce_fusion.9), channel_id=1, replica_groups=mesh['pairs'=1,'rows'=8] {'rows'}, use_global_device_ids=true, to_apply=%region_4.0 | all-reduce | flops 2048 | bytes 16384 | tf_op jit(solution)/shard_map/while/body/eval_jaxpr/psum | solution.py:18
  337.4 23.1 %psum.18 = f32[2048]{0:T(1024)S(1)} all-reduce(f32[2048]{0:T(1024)S(1)} %multiply_reduce_fusion.9), channel_id=1, replica_groups=mesh['pairs'=1,'rows'=8] {'rows'}, use_global_device_ids=true, to_apply=%region_4.0 | all-reduce | flops 2048 | bytes 16384 | tf_op jit(solution)/shard_map/while/body/eval_jaxpr/psum | solution.py:18
  361.0 24.1 %psum.18 = f32[2048]{0:T(1024)S(1)} all-reduce(f32[2048]{0:T(1024)S(1)} %multiply_reduce_fusion.9), channel_id=1, replica_groups=mesh['pairs'=1,'rows'=8] {'rows'}, use_global_device_ids=true, to_apply=%region_4.0 | all-reduce | flops 2048 | bytes 16384 | tf_op jit(solution)/shard_map/while/body/eval_jaxpr/psum | solution.py:18
  385.1 3.3 multiply_convert_fusion
  388.5 49.3 %all-gather.11.cloned.1.call-done = bf16[2048,2048]{1,0:T(8,128)(2,1)} async-done(((bf16[256,2048]{1,0:T(8,128)(2,1)}), bf16[2048,2048]{1,0:T(8,128)(2,1)}) %all-gather.11.cloned.1.call-update) | async-done | bytes 8388624 | tf_op jit(solution)/shard_map/all_gather | solution.py:34
  437.8 16.4 %fusion.8 = (f32[256]{0:T(256)S(1)}, f32[256,2048]{1,0:T(8,128)}) fusion(f32[256,2048]{1,0:T(8,128)S(1)} %copy-done.2, bf16[2048,2048]{1,0:T(8,128)(2,1)} %all-gather.9.cloned.1.call-done, bf16[2048,2048]{1,0:T(8,128)(2,1)} %all-gather.11.cloned.1.call-done, f32[256,2048]{1,0:T(8,128)} %param.12), kind=kOutput, calls=%fused_computation.19 | convolution fusion | flops 4297064448 | bytes 23069696 | tf_op jit(solution)/shard_map/dot_general | solution.py:37
  456.8 240.3 %while.27 = (s32[]{:T(128)}, f32[256]{0:T(256)}, f32[2048]{0:T(1024)S(1)}, f32[256,2048]{1,0:T(8,128)S(1)}, f32[256]{0:T(256)S(1)}, /*index=5*/f32[2048]{0:T(1024)S(1)}, s32[]{:T(128)}, s32[]{:T(128)}) while((s32[]{:T(128)}, f32[256]{0:T(256)}, f32[2048]{0:T(1024)S(1)}, f32[256,2048]{1,0:T(8,128)S(1)}, f32[256]{0:T(256)S(1)}, ...), condition=%wide.region_11.0_spmd.clone, body=%wide.region_7.0_spmd.clone.sunk | while | flops 2101251 | bytes 4277371 | solution.py:21
  457.3 22.3 %psum.19 = f32[2048]{0:T(1024)S(1)} all-reduce(f32[2048]{0:T(1024)S(1)} %multiply_reduce_fusion.11), channel_id=1, replica_groups=mesh['pairs'=1,'rows'=8] {'rows'}, use_global_device_ids=true, to_apply=%region_10.0 | all-reduce | flops 2048 | bytes 16384 | tf_op jit(solution)/shard_map/while/body/eval_jaxpr/psum | solution.py:18
  480.1 24.1 %psum.19 = f32[2048]{0:T(1024)S(1)} all-reduce(f32[2048]{0:T(1024)S(1)} %multiply_reduce_fusion.11), channel_id=1, replica_groups=mesh['pairs'=1,'rows'=8] {'rows'}, use_global_device_ids=true, to_apply=%region_10.0 | all-reduce | flops 2048 | bytes 16384 | tf_op jit(solution)/shard_map/while/body/eval_jaxpr/psum | solution.py:18
  504.7 23.1 %psum.19 = f32[2048]{0:T(1024)S(1)} all-reduce(f32[2048]{0:T(1024)S(1)} %multiply_reduce_fusion.11), channel_id=1, replica_groups=mesh['pairs'=1,'rows'=8] {'rows'}, use_global_device_ids=true, to_apply=%region_10.0 | all-reduce | flops 2048 | bytes 16384 | tf_op jit(solution)/shard_map/while/body/eval_jaxpr/psum | solution.py:18
  528.3 24.1 %psum.19 = f32[2048]{0:T(1024)S(1)} all-reduce(f32[2048]{0:T(1024)S(1)} %multiply_reduce_fusion.11), channel_id=1, replica_groups=mesh['pairs'=1,'rows'=8] {'rows'}, use_global_device_ids=true, to_apply=%region_10.0 | all-reduce | flops 2048 | bytes 16384 | tf_op jit(solution)/shard_map/while/body/eval_jaxpr/psum | solution.py:18
  552.9 23.1 %psum.19 = f32[2048]{0:T(1024)S(1)} all-reduce(f32[2048]{0:T(1024)S(1)} %multiply_reduce_fusion.11), channel_id=1, replica_groups=mesh['pairs'=1,'rows'=8] {'rows'}, use_global_device_ids=true, to_apply=%region_10.0 | all-reduce | flops 2048 | bytes 16384 | tf_op jit(solution)/shard_map/while/body/eval_jaxpr/psum | solution.py:18
  576.5 24.1 %psum.19 = f32[2048]{0:T(1024)S(1)} all-reduce(f32[2048]{0:T(1024)S(1)} %multiply_reduce_fusion.11), channel_id=1, replica_groups=mesh['pairs'=1,'rows'=8] {'rows'}, use_global_device_ids=true, to_apply=%region_10.0 | all-reduce | flops 2048 | bytes 16384 | tf_op jit(solution)/shard_map/while/body/eval_jaxpr/psum | solution.py:18
  601.1 23.1 %psum.19 = f32[2048]{0:T(1024)S(1)} all-reduce(f32[2048]{0:T(1024)S(1)} %multiply_reduce_fusion.11), channel_id=1, replica_groups=mesh['pairs'=1,'rows'=8] {'rows'}, use_global_device_ids=true, to_apply=%region_10.0 | all-reduce | flops 2048 | bytes 16384 | tf_op jit(solution)/shard_map/while/body/eval_jaxpr/psum | solution.py:18
  624.8 24.1 %psum.19 = f32[2048]{0:T(1024)S(1)} all-reduce(f32[2048]{0:T(1024)S(1)} %multiply_reduce_fusion.11), channel_id=1, replica_groups=mesh['pairs'=1,'rows'=8] {'rows'}, use_global_device_ids=true, to_apply=%region_10.0 | all-reduce | flops 2048 | bytes 16384 | tf_op jit(solution)/shard_map/while/body/eval_jaxpr/psum | solution.py:18
  649.3 23.1 %psum.19 = f32[2048]{0:T(1024)S(1)} all-reduce(f32[2048]{0:T(1024)S(1)} %multiply_reduce_fusion.11), channel_id=1, replica_groups=mesh['pairs'=1,'rows'=8] {'rows'}, use_global_device_ids=true, to_apply=%region_10.0 | all-reduce | flops 2048 | bytes 16384 | tf_op jit(solution)/shard_map/while/body/eval_jaxpr/psum | solution.py:18
  673.0 24.1 %psum.19 = f32[2048]{0:T(1024)S(1)} all-reduce(f32[2048]{0:T(1024)S(1)} %multiply_reduce_fusion.11), channel_id=1, replica_groups=mesh['pairs'=1,'rows'=8] {'rows'}, use_global_device_ids=true, to_apply=%region_10.0 | all-reduce | flops 2048 | bytes 16384 | tf_op jit(solution)/shard_map/while/body/eval_jaxpr/psum | solution.py:18
  697.1 3.5 multiply_multiply_fusion
  (168 shorter events, 17.1 us)
Async XLA Ops:
  6.5 23.0 %all-gather.5.cloned.1.call-start = ((), (), s32[]{:S(2)}) async-start(), calls=%async_computation | async-start | bytes 1179648 | tf_op jit(solution)/shard_map/all_gather | solution.py:29
  8.2 3.1 copy-start
  8.2 71.6 %all-gather.9.cloned.1.call-start = ((), (), s32[]{:S(2)}) async-start(), calls=%async_computation.2 | async-start | bytes 9437184 | tf_op jit(solution)/shard_map/all_gather | solution.py:35
  11.2 18.4 %copy-start.4 = (f32[256,256]{1,0:T(8,128)S(1)}, f32[256,256]{1,0:T(8,128)}, u32[]{:S(2)}) copy-start(f32[256,256]{1,0:T(8,128)} %param.17) | copy-start | bytes 786436
  11.2 118.7 %all-gather.7.cloned.1.call-start = ((), (), s32[]{:S(2)}) async-start(), calls=%async_computation.1 | async-start | bytes 9437184 | tf_op jit(solution)/shard_map/all_gather | solution.py:34
  12.4 425.4 %all-gather.11.cloned.1.call-start = ((), (), s32[]{:S(2)}) async-start(), calls=%async_computation.3 | async-start | bytes 9437184 | tf_op jit(solution)/shard_map/all_gather | solution.py:34
  31.3 111.0 %copy-start.1 = (f32[256,2048]{1,0:T(8,128)}, f32[256,2048]{1,0:T(8,128)S(1)}, u32[]{:S(2)}) copy-start(f32[256,2048]{1,0:T(8,128)S(1)} %convolution_multiply_fusion) | copy-start | bytes 6291460
  142.2 2.6 copy-start.3
  142.2 2.6 copy-start.5
  145.1 22.6 %copy-start.6 = (f32[256]{0:T(256)}, f32[256]{0:T(256)S(1)}, u32[]{:S(2)}) copy-start(f32[256]{0:T(256)S(1)} %div.53) | copy-start | bytes 3076 | tf_op jit(solution)/shard_map/while
  167.9 24.3 %copy-start.6 = (f32[256]{0:T(256)}, f32[256]{0:T(256)S(1)}, u32[]{:S(2)}) copy-start(f32[256]{0:T(256)S(1)} %div.53) | copy-start | bytes 3076 | tf_op jit(solution)/shard_map/while
  192.4 23.4 %copy-start.6 = (f32[256]{0:T(256)}, f32[256]{0:T(256)S(1)}, u32[]{:S(2)}) copy-start(f32[256]{0:T(256)S(1)} %div.53) | copy-start | bytes 3076 | tf_op jit(solution)/shard_map/while
  216.1 24.3 %copy-start.6 = (f32[256]{0:T(256)}, f32[256]{0:T(256)S(1)}, u32[]{:S(2)}) copy-start(f32[256]{0:T(256)S(1)} %div.53) | copy-start | bytes 3076 | tf_op jit(solution)/shard_map/while
  240.7 23.4 %copy-start.6 = (f32[256]{0:T(256)}, f32[256]{0:T(256)S(1)}, u32[]{:S(2)}) copy-start(f32[256]{0:T(256)S(1)} %div.53) | copy-start | bytes 3076 | tf_op jit(solution)/shard_map/while
  264.3 24.3 %copy-start.6 = (f32[256]{0:T(256)}, f32[256]{0:T(256)S(1)}, u32[]{:S(2)}) copy-start(f32[256]{0:T(256)S(1)} %div.53) | copy-start | bytes 3076 | tf_op jit(solution)/shard_map/while
  288.9 23.4 %copy-start.6 = (f32[256]{0:T(256)}, f32[256]{0:T(256)S(1)}, u32[]{:S(2)}) copy-start(f32[256]{0:T(256)S(1)} %div.53) | copy-start | bytes 3076 | tf_op jit(solution)/shard_map/while
  312.6 24.3 %copy-start.6 = (f32[256]{0:T(256)}, f32[256]{0:T(256)S(1)}, u32[]{:S(2)}) copy-start(f32[256]{0:T(256)S(1)} %div.53) | copy-start | bytes 3076 | tf_op jit(solution)/shard_map/while
  337.1 23.4 %copy-start.6 = (f32[256]{0:T(256)}, f32[256]{0:T(256)S(1)}, u32[]{:S(2)}) copy-start(f32[256]{0:T(256)S(1)} %div.53) | copy-start | bytes 3076 | tf_op jit(solution)/shard_map/while
  360.8 24.3 %copy-start.6 = (f32[256]{0:T(256)}, f32[256]{0:T(256)S(1)}, u32[]{:S(2)}) copy-start(f32[256]{0:T(256)S(1)} %div.53) | copy-start | bytes 3076 | tf_op jit(solution)/shard_map/while
  385.1 52.7 %copy-start.2 = (f32[256,2048]{1,0:T(8,128)S(1)}, f32[256,2048]{1,0:T(8,128)}, u32[]{:S(2)}) copy-start(f32[256,2048]{1,0:T(8,128)} %copy-done.1) | copy-start | bytes 6291460
  457.0 22.6 %copy-start.7 = (f32[256]{0:T(256)}, f32[256]{0:T(256)S(1)}, u32[]{:S(2)}) copy-start(f32[256]{0:T(256)S(1)} %div.55) | copy-start | bytes 3076 | tf_op jit(solution)/shard_map/while
  479.9 24.3 %copy-start.7 = (f32[256]{0:T(256)}, f32[256]{0:T(256)S(1)}, u32[]{:S(2)}) copy-start(f32[256]{0:T(256)S(1)} %div.55) | copy-start | bytes 3076 | tf_op jit(solution)/shard_map/while
  504.4 23.4 %copy-start.7 = (f32[256]{0:T(256)}, f32[256]{0:T(256)S(1)}, u32[]{:S(2)}) copy-start(f32[256]{0:T(256)S(1)} %div.55) | copy-start | bytes 3076 | tf_op jit(solution)/shard_map/while
  528.1 24.3 %copy-start.7 = (f32[256]{0:T(256)}, f32[256]{0:T(256)S(1)}, u32[]{:S(2)}) copy-start(f32[256]{0:T(256)S(1)} %div.55) | copy-start | bytes 3076 | tf_op jit(solution)/shard_map/while
  552.6 23.4 %copy-start.7 = (f32[256]{0:T(256)}, f32[256]{0:T(256)S(1)}, u32[]{:S(2)}) copy-start(f32[256]{0:T(256)S(1)} %div.55) | copy-start | bytes 3076 | tf_op jit(solution)/shard_map/while
  576.3 24.3 %copy-start.7 = (f32[256]{0:T(256)}, f32[256]{0:T(256)S(1)}, u32[]{:S(2)}) copy-start(f32[256]{0:T(256)S(1)} %div.55) | copy-start | bytes 3076 | tf_op jit(solution)/shard_map/while
  600.9 23.4 %copy-start.7 = (f32[256]{0:T(256)}, f32[256]{0:T(256)S(1)}, u32[]{:S(2)}) copy-start(f32[256]{0:T(256)S(1)} %div.55) | copy-start | bytes 3076 | tf_op jit(solution)/shard_map/while
  624.5 24.3 %copy-start.7 = (f32[256]{0:T(256)}, f32[256]{0:T(256)S(1)}, u32[]{:S(2)}) copy-start(f32[256]{0:T(256)S(1)} %div.55) | copy-start | bytes 3076 | tf_op jit(solution)/shard_map/while
  649.1 23.4 %copy-start.7 = (f32[256]{0:T(256)}, f32[256]{0:T(256)S(1)}, u32[]{:S(2)}) copy-start(f32[256]{0:T(256)S(1)} %div.55) | copy-start | bytes 3076 | tf_op jit(solution)/shard_map/while
  672.8 24.3 %copy-start.7 = (f32[256]{0:T(256)}, f32[256]{0:T(256)S(1)}, u32[]{:S(2)}) copy-start(f32[256]{0:T(256)S(1)} %div.55) | copy-start | bytes 3076 | tf_op jit(solution)/shard_map/while
Sparse Core Ops, SparseCore 0:
  9.1 20.3 all-gather.4
  31.4 48.3 all-gather.8
  81.6 48.3 all-gather.6
  388.6 49.1 all-gather.10
where the time goes:
time: 711 us; the launch traced here: 707 us
  blocking collectives  470 us (66%)
  waiting for transfers between devices  164 us (23%)
  matrix products  30.4 us (4%)
  other arithmetic  25.8 us (4%)
  between operations  13.9 us (2%)
    psum x20, blocking collectives, value_a14(): col_sum = lax.psum(jnp.sum(kernel * row_scale[:, None], axis=0), 'rows')  470 us
    all_gather x2, waiting for transfers between devices, local_fgw(): lax.all_gather(transport.astype(jnp.bfloat16), 'rows', tiled=True)  99.5 us
    all_gather x1, waiting for transfers between devices, local_fgw(): tgt_all = lax.all_gather(tgt_half, 'rows', tiled=True)  48.5 us
    dot_general x2, matrix products, local_fgw(): jnp.dot(prod_a.astype(jnp.bfloat16), tgt_all, preferred_element_type=jnp....  28.7 us
    all_gather x1, waiting for transfers between devices, local_fgw(): feat_all = lax.all_gather(feat_tgt.astype(jnp.bfloat16), 'rows', tiled=True)  16.4 us
  transfers between devices with their start and end apart: 4, of which 4 were waited for; matrix products, arithmetic and copies ran while one was open for 1% of the time, Pallas kernels for 0%

commit v1 on v0

v1 whole, which is shorter than its diff:
```python
import functools

import jax
import jax.numpy as jnp
from jax import lax
from jax.experimental import pallas as pl
from jax.experimental.pallas import tpu as pltpu
from jax.sharding import PartitionSpec as P

ALPHA = 0.5
OUTER_STEPS = 2
SWEEPS = 10
LANES = 128
SUB = 8


def entry_barrier(me, n):
    barrier = pltpu.get_barrier_semaphore()
    for off in range(1, n):
        pl.semaphore_signal(barrier, inc=1, device_id={"rows": lax.rem(me + off, n)})
    pl.semaphore_wait(barrier, n - 1)


def build_kernel(cost_ref, kern_ref, eps, rows, cols):
    tiles = cols // LANES

    def block(b, carry):
        row = pl.multiple_of(b * SUB, SUB)
        vals = [cost_ref[pl.ds(row, SUB), t * LANES:(t + 1) * LANES] for t in range(tiles)]
        low = functools.reduce(jnp.minimum, vals)
        low = jnp.min(low, axis=1, keepdims=True)
        for t in range(tiles):
            kern_ref[pl.ds(row, SUB), t * LANES:(t + 1) * LANES] = jnp.exp((low - vals[t]) / eps)
        return carry

    lax.fori_loop(0, rows // SUB, block, 0, unroll=4)


def tree_sum(vals):
    while len(vals) > 1:
        vals = [a + b for a, b in zip(vals[::2], vals[1::2])] + vals[len(vals) & ~1:]
    return vals[0]


def sinkhorn(me, n, kern_ref, p_ref, q_ref, u_ref, v_ref, part_ref, gath_ref, send_sem, recv_sem, rows, cols, first):
    tiles = cols // LANES
    blocks = rows // SUB

    def copy(par, peer, slot):
        return pltpu.make_async_remote_copy(
            src_ref=part_ref.at[par], dst_ref=gath_ref.at[par, slot],
            send_sem=send_sem.at[par, peer], recv_sem=recv_sem.at[par, slot], device_id={"rows": peer})

    v_ref[...] = jnp.ones_like(v_ref)

    def sweep(step, carry):
        par = lax.rem(step + first, 2)
        vrow = [jnp.broadcast_to(v_ref[t:t + 1, :], (SUB, LANES)) for t in range(tiles)]
        for b in range(blocks):
            prods = [kern_ref[b * SUB:(b + 1) * SUB, t * LANES:(t + 1) * LANES] * vrow[t] for t in range(tiles)]
            dots = jnp.sum(tree_sum(prods), axis=1, keepdims=True)
            u_ref[b * SUB:(b + 1) * SUB, :] = p_ref[b * SUB:(b + 1) * SUB, :] / dots
        acc = [None] * tiles
        for b in range(blocks):
            scale = u_ref[b * SUB:(b + 1) * SUB, :]
            for t in range(tiles):
                term = kern_ref[b * SUB:(b + 1) * SUB, t * LANES:(t + 1) * LANES] * scale
                acc[t] = term if acc[t] is None else acc[t] + term
        sums = jnp.concatenate([jnp.sum(a, axis=0, keepdims=True) for a in acc], axis=0)
        part_ref[par] = sums
        gath_ref[par, me] = sums
        for off in range(1, n):
            copy(par, lax.rem(me + off, n), me).start()
        for off in range(1, n):
            copy(par, lax.rem(me + off, n), lax.rem(me + off, n)).wait_recv()
        total = gath_ref[par, 0]
        for d in range(1, n):
            total = total + gath_ref[par, d]
        v_ref[...] = q_ref[...] / total
        for off in range(1, n):
            copy(par, lax.rem(me + off, n), me).wait_send()
        return carry

    lax.fori_loop(0, SWEEPS, sweep, 0)


def write_plan(kern_ref, u_ref, v_ref, out_ref, rows, cols):
    tiles = cols // LANES
    vrow = [jnp.broadcast_to(v_ref[t:t + 1, :], (SUB, LANES)) for t in range(tiles)]

    def block(b, carry):
        row = pl.multiple_of(b * SUB, SUB)
        scale = u_ref[pl.ds(row, SUB), :]
        for t in range(tiles):
            out_ref[pl.ds(row, SUB), t * LANES:(t + 1) * LANES] = scale * kern_ref[pl.ds(row, SUB), t * LANES:(t + 1) * LANES] * vrow[t]
        return carry

    lax.fori_loop(0, rows // SUB, block, 0, unroll=4)


def sinkhorn_kernel(n, eps_ref, cost_ref, p_ref, q_ref, out_ref, kern_ref, u_ref, v_ref, part_ref, gath_ref, send_sem, recv_sem):
    me = lax.axis_index("rows")
    rows, cols = cost_ref.shape
    entry_barrier(me, n)
    build_kernel(cost_ref, kern_ref, eps_ref[0], rows, cols)
    sinkhorn(me, n, kern_ref, p_ref, q_ref, u_ref, v_ref, part_ref, gath_ref, send_sem, recv_sem, rows, cols, 0)
    write_plan(kern_ref, u_ref, v_ref, out_ref, rows, cols)


def scaled_plan(n, cid, cost, p_wide, q_tiles, eps):
    rows, cols = cost.shape
    tiles = cols // LANES
    vmem = pl.BlockSpec(memory_space=pltpu.VMEM)
    return pl.pallas_call(
        functools.partial(sinkhorn_kernel, n),
        out_shape=jax.ShapeDtypeStruct((rows, cols), jnp.float32),
        in_specs=[pl.BlockSpec(memory_space=pltpu.SMEM), vmem, vmem, vmem],
        out_specs=vmem,
        scratch_shapes=[
            pltpu.VMEM((rows, cols), jnp.float32),
            pltpu.VMEM((rows, LANES), jnp.float32),
            pltpu.VMEM((tiles, LANES), jnp.float32),
            pltpu.VMEM((2, tiles, LANES), jnp.float32),
            pltpu.VMEM((2, n, tiles, LANES), jnp.float32),
            pltpu.SemaphoreType.DMA((2, n)),
            pltpu.SemaphoreType.DMA((2, n)),
        ],
        compiler_params=pltpu.CompilerParams(collective_id=cid, has_side_effects=True, vmem_limit_bytes=32 << 20),
        name="scaled_plan",
    )(eps, cost, p_wide, q_tiles)


def solution(mesh):
    n = mesh.shape["rows"]

    def local_fgw(cost_src, cost_tgt, plan_init, mass_src, mass_tgt, feat_src, feat_tgt, epsilon):
        src_half = cost_src.astype(jnp.bfloat16)
        tgt_half = cost_tgt.astype(jnp.bfloat16)
        feat_all = lax.all_gather(feat_tgt.astype(jnp.bfloat16), 'rows', tiled=True)
        cross_term = jnp.einsum('id,jd->ij', feat_src.astype(jnp.bfloat16), feat_all, preferred_element_type=jnp.float32)
        feat_cost = (-2.0 * ALPHA) * cross_term
        p_wide = jnp.broadcast_to(mass_src[:, None], (mass_src.shape[0], LANES))
        q_tiles = mass_tgt.reshape(-1, LANES)
        eps = epsilon.reshape(1)
        transport = plan_init
        for step_index in range(OUTER_STEPS):
            transport_all = lax.all_gather(transport.astype(jnp.bfloat16), 'rows', tiled=True)
            tgt_all = lax.all_gather(tgt_half, 'rows', tiled=True)
            prod_a = jnp.dot(src_half, transport_all, preferred_element_type=jnp.float32)
            prod_b = jnp.dot(prod_a.astype(jnp.bfloat16), tgt_all, preferred_element_type=jnp.float32)
            step_cost = feat_cost - (2.0 * (1.0 - ALPHA)) * prod_b
            transport = scaled_plan(n, 0, step_cost, p_wide, q_tiles, eps)
        return transport

    row_spec = P(('pairs', 'rows'), None)
    vec_spec = P(('pairs', 'rows'))
    in_specs = (row_spec, row_spec, row_spec, vec_spec, P('pairs'), row_spec, row_spec, P())
    return jax.shard_map(local_fgw, mesh=mesh, in_specs=in_specs, out_specs=row_spec, check_vma=False)
```

time: 711 us -> 292 us (0.41)
  blocking collectives: 470 us -> 0 us
  Pallas kernels: 0 us -> 76.9 us
  other arithmetic: 25.8 us -> 6.75 us
    psum x20 -> x0, blocking collectives: 470 us -> none  [value_a14(): col_sum = lax.psum(jnp.sum(kernel * row_scale[:, None], axis=0), 'rows')]
    pallas_call x0 -> x2, Pallas kernels: none -> 76.9 us  [scaled_plan(): pl.pallas_call(functools.partial(sinkhorn_kernel, n), out_shape=jax.Shape...]
    reduce_sum x40 -> x0, other arithmetic: 8.95 us -> none  [the longest x20 4.61 us: value_a14(): row_scale = mass_rows / jnp.sum(kernel * scales[1][None, :], axis=1)]
  transfers between devices with their start and end apart: 4 -> 4, of which waited for: 4 -> 4; matrix products, arithmetic and copies ran while one was open for 1% -> 2% of each run, Pallas kernels for 0% -> 0%
where the time goes in v1:
time: 292 us
  waiting for transfers between devices  162 us (55%)
  Pallas kernels  76.9 us (26%)
  matrix products  30.2 us (10%)
  between operations  13.9 us (5%)
  other arithmetic  6.75 us (2%)
    all_gather x2, waiting for transfers between devices, local_fgw(): lax.all_gather(transport.astype(jnp.bfloat16), 'rows', tiled=True)  98.7 us
    pallas_call x2, Pallas kernels, scaled_plan(): pl.pallas_call(functools.partial(sinkhorn_kernel, n), out_shape=jax.Shape...  76.9 us
    all_gather x1, waiting for transfers between devices, local_fgw(): tgt_all = lax.all_gather(tgt_half, 'rows', tiled=True)  47.2 us
    dot_general x2, matrix products, local_fgw(): jnp.dot(prod_a.astype(jnp.bfloat16), tgt_all, preferred_element_type=jnp....  27.2 us
    all_gather x1, waiting for transfers between devices, local_fgw(): feat_all = lax.all_gather(feat_tgt.astype(jnp.bfloat16), 'rows', tiled=True)  16.5 us
  transfers between devices with their start and end apart: 4, of which 4 were waited for; matrix products, arithmetic and copies ran while one was open for 2% of the time, Pallas kernels for 0%

profile of v1, /device:TPU:0, one launch (start us, length us, event | category | flops | bytes accessed | tf_op | source)
XLA Modules:
  0.0 291.6 jit_solution(12455241304651489680)
XLA Ops:
  6.5 0.0 all-gather.5.cloned.1.call-start
  6.5 1.6 convert_element_type.26
  8.2 0.0 all-gather.5.cloned.1.call-update
  8.2 0.0 copy-start.1
  8.2 0.0 all-gather.9.cloned.1.call-start
  8.2 2.9 convert_element_type.30
  11.1 0.0 all-gather.9.cloned.1.call-update
  11.1 0.0 copy-start.2
  11.2 0.0 all-gather.7.cloned.1.call-start
  11.2 0.0 copy-done.1
  11.2 1.1 convert_element_type.28
  12.3 0.0 all-gather.7.cloned.1.call-update
  12.4 0.0 all-gather.11.cloned.1.call-start
  13.1 16.5 %all-gather.5.cloned.1.call-done = bf16[2048,256]{1,0:T(8,128)(2,1)} async-done(((bf16[256,256]{1,0:T(8,128)(2,1)}), bf16[2048,256]{1,0:T(8,128)(2,1)}) %all-gather.5.cloned.1.call-update) | async-done | bytes 1048592 | tf_op jit(solution)/shard_map/all_gather | solution.py:139
  29.6 0.0 copy-done.2
  29.6 3.0 %convolution_multiply_fusion = f32[256,2048]{1,0:T(8,128)} fusion(bf16[2048,256]{1,0:T(8,128)(2,1)} %all-gather.5.cloned.1.call-done, f32[256,256]{1,0:T(8,128)S(1)} %copy-done.2), kind=kOutput, calls=%fused_computation | convolution fusion | flops 269025280 | bytes 3407872 | tf_op jit(solution)/shard_map/id,jd->ij/dot_general | solution.py:140
  32.6 0.0 copy-start.3
  32.6 0.0 copy-start
  32.6 47.2 %all-gather.9.cloned.1.call-done = bf16[2048,2048]{1,0:T(8,128)(2,1)} async-done(((bf16[256,2048]{1,0:T(8,128)(2,1)}), bf16[2048,2048]{1,0:T(8,128)(2,1)}) %all-gather.9.cloned.1.call-update) | async-done | bytes 8388624 | tf_op jit(solution)/shard_map/all_gather | solution.py:148
  79.7 50.2 %all-gather.7.cloned.1.call-done = bf16[2048,2048]{1,0:T(8,128)(2,1)} async-done(((bf16[256,2048]{1,0:T(8,128)(2,1)}), bf16[2048,2048]{1,0:T(8,128)(2,1)}) %all-gather.7.cloned.1.call-update) | async-done | bytes 8388624 | tf_op jit(solution)/shard_map/all_gather | solution.py:147
  129.9 11.5 %convolution_subtract_fusion.1.cost_ref = f32[256,2048]{1,0:T(8,128)S(1)} fusion(f32[256,2048]{1,0:T(8,128)} %convolution_multiply_fusion, bf16[2048,2048]{1,0:T(8,128)(2,1)} %all-gather.9.cloned.1.call-done, bf16[2048,2048]{1,0:T(8,128)(2,1)} %all-gather.7.cloned.1.call-done, f32[256,2048]{1,0:T(8,128)} %param.8), kind=kOutput, calls=%fused_computation.2 | convolution fusion | flops 4296540160 | bytes 23068672 | tf_op jit(solution)/shard_map/dot_general | solution.py:150
  141.4 0.0 copy-done.3
  141.4 0.1 broadcast_in_dim.2.p_ref
  141.5 0.0 copy-done
  141.5 38.4 %scaled_plan.2 = f32[256,2048]{1,0:T(8,128)S(1)} custom-call(f32[1]{0:T(128)} %bitcast.7.eps_ref, f32[256,2048]{1,0:T(8,128)S(1)} %convolution_subtract_fusion.1.cost_ref, f32[256,128]{1,0:T(8,128)S(1)} %broadcast_in_dim.2.p_ref, f32[16,128]{1,0:T(8,128)S(1)} %bitcast.9), custom_call_target="tpu_custom_call" | custom-call | tf_op jit(solution)/shard_map/scaled_plan/pallas_call | solution.py:114
  180.0 1.1 convert_element_type.31
  181.1 0.0 all-gather.11.cloned.1.call-update
  181.1 48.5 %all-gather.11.cloned.1.call-done = bf16[2048,2048]{1,0:T(8,128)(2,1)} async-done(((bf16[256,2048]{1,0:T(8,128)(2,1)}), bf16[2048,2048]{1,0:T(8,128)(2,1)}) %all-gather.11.cloned.1.call-update) | async-done | bytes 8388624 | tf_op jit(solution)/shard_map/all_gather | solution.py:147
  229.6 15.7 %convolution_subtract_fusion.cost_ref = f32[256,2048]{1,0:T(8,128)S(1)} fusion(f32[256,2048]{1,0:T(8,128)} %convolution_multiply_fusion, bf16[2048,2048]{1,0:T(8,128)(2,1)} %all-gather.9.cloned.1.call-done, bf16[2048,2048]{1,0:T(8,128)(2,1)} %all-gather.11.cloned.1.call-done, f32[256,2048]{1,0:T(8,128)} %param.8), kind=kOutput, calls=%fused_computation.1 | convolution fusion | flops 4296540160 | bytes 23068672 | tf_op jit(solution)/shard_map/dot_general | solution.py:150
  245.3 38.4 %scaled_plan.3 = f32[256,2048]{1,0:T(8,128)S(1)} custom-call(f32[1]{0:T(128)} %bitcast.8.eps_ref, f32[256,2048]{1,0:T(8,128)S(1)} %convolution_subtract_fusion.cost_ref, f32[256,128]{1,0:T(8,128)S(1)} %broadcast_in_dim.2.p_ref, f32[16,128]{1,0:T(8,128)S(1)} %bitcast.10), custom_call_target="tpu_custom_call" | custom-call | tf_op jit(solution)/shard_map/scaled_plan/pallas_call | solution.py:114
  283.8 1.3 copy.11
Async XLA Ops:
  6.5 23.0 %all-gather.5.cloned.1.call-start = ((), (), s32[]{:S(2)}) async-start(), calls=%async_computation | async-start | bytes 1179648 | tf_op jit(solution)/shard_map/all_gather | solution.py:139
  8.2 3.0 %copy-start.1 = (f32[256,2048]{1,0:T(8,128)S(1)}, f32[256,2048]{1,0:T(8,128)}, u32[]{:S(2)}) copy-start(f32[256,2048]{1,0:T(8,128)} %param.10) | copy-start | bytes 6291460
  8.2 71.6 %all-gather.9.cloned.1.call-start = ((), (), s32[]{:S(2)}) async-start(), calls=%async_computation.2 | async-start | bytes 9437184 | tf_op jit(solution)/shard_map/all_gather | solution.py:148
  11.1 18.4 %copy-start.2 = (f32[256,256]{1,0:T(8,128)S(1)}, f32[256,256]{1,0:T(8,128)}, u32[]{:S(2)}) copy-start(f32[256,256]{1,0:T(8,128)} %param.13) | copy-start | bytes 786436
  11.2 118.8 %all-gather.7.cloned.1.call-start = ((), (), s32[]{:S(2)}) async-start(), calls=%async_computation.1 | async-start | bytes 9437184 | tf_op jit(solution)/shard_map/all_gather | solution.py:147
  12.4 217.2 %all-gather.11.cloned.1.call-start = ((), (), s32[]{:S(2)}) async-start(), calls=%async_computation.3 | async-start | bytes 9437184 | tf_op jit(solution)/shard_map/all_gather | solution.py:147
  32.6 108.8 %copy-start.3 = (f32[256]{0:T(256)S(1)}, f32[256]{0:T(256)}, u32[]{:S(2)}) copy-start(f32[256]{0:T(256)} %param.11) | copy-start | bytes 3076
  32.6 108.9 %copy-start = (f32[2048]{0:T(1024)S(1)}, f32[2048]{0:T(1024)}, u32[]{:S(2)}) copy-start(f32[2048]{0:T(1024)} %param.12) | copy-start | bytes 24580
Sparse Core Ops, SparseCore 0:
  9.1 20.3 all-gather.4
  31.4 48.3 all-gather.8
  81.6 48.3 all-gather.6
  181.2 48.3 all-gather.10

commit v2 on v1

v2 whole, which is shorter than its diff:
```python
import functools

import jax
import jax.numpy as jnp
from jax import lax
from jax.experimental import pallas as pl
from jax.experimental.pallas import tpu as pltpu
from jax.sharding import PartitionSpec as P

ALPHA = 0.5
OUTER_STEPS = 2
SWEEPS = 10
LANES = 128
SUB = 8
BLK = 256
DEV = 8
AHEAD = 2
LAG = 2


def tree_sum(vals):
    while len(vals) > 1:
        vals = [a + b for a, b in zip(vals[::2], vals[1::2])] + vals[len(vals) & ~1:]
    return vals[0]


def rows_of(owner):
    return pl.ds(pl.multiple_of(owner * BLK, BLK), BLK)


class Place:
    def __init__(self):
        self.me = lax.axis_index("rows")
        core = lax.rem(self.me, 2)
        x = lax.rem(self.me // 2, 2)
        y = self.me // 4
        self.core = core
        self.sib = self.me + 1 - 2 * core
        dx, dy = 2 - 4 * x, 4 - 8 * y
        self.x0, self.x1 = self.me + dx, self.sib + dx
        self.y0, self.y1 = self.me + dy, self.sib + dy
        self.d0, self.d1 = self.me + dx + dy, self.sib + dx + dy


def build_kernel(cost_ref, kern_ref, eps, rows, cols):
    tiles = cols // LANES

    def block(b, carry):
        row = pl.multiple_of(b * SUB, SUB)
        vals = [cost_ref[pl.ds(row, SUB), t * LANES:(t + 1) * LANES] for t in range(tiles)]
        low = functools.reduce(jnp.minimum, vals)
        low = jnp.min(low, axis=1, keepdims=True)
        for t in range(tiles):
            kern_ref[pl.ds(row, SUB), t * LANES:(t + 1) * LANES] = jnp.exp((low - vals[t]) / eps)
        return carry

    lax.fori_loop(0, rows // SUB, block, 0, unroll=4)


def sinkhorn(at, kern_ref, p_ref, q_ref, u_ref, v_ref, part_ref, gath_ref, send_sem, recv_sem, rows, cols):
    tiles = cols // LANES
    blocks = rows // SUB
    me = at.me

    def copy(par, peer, slot):
        return pltpu.make_async_remote_copy(
            src_ref=part_ref.at[par], dst_ref=gath_ref.at[par, slot],
            send_sem=send_sem.at[par, peer], recv_sem=recv_sem.at[par, slot], device_id={"rows": peer})

    v_ref[...] = jnp.ones_like(v_ref)

    def sweep(step, carry):
        par = lax.rem(step, 2)
        vrow = [jnp.broadcast_to(v_ref[t:t + 1, :], (SUB, LANES)) for t in range(tiles)]
        for b in range(blocks):
            prods = [kern_ref[b * SUB:(b + 1) * SUB, t * LANES:(t + 1) * LANES] * vrow[t] for t in range(tiles)]
            dots = jnp.sum(tree_sum(prods), axis=1, keepdims=True)
            u_ref[b * SUB:(b + 1) * SUB, :] = p_ref[b * SUB:(b + 1) * SUB, :] / dots
        acc = [None] * tiles
        for b in range(blocks):
            scale = u_ref[b * SUB:(b + 1) * SUB, :]
            for t in range(tiles):
                term = kern_ref[b * SUB:(b + 1) * SUB, t * LANES:(t + 1) * LANES] * scale
                acc[t] = term if acc[t] is None else acc[t] + term
        sums = jnp.concatenate([jnp.sum(a, axis=0, keepdims=True) for a in acc], axis=0)
        part_ref[par] = sums
        gath_ref[par, me] = sums
        for off in range(1, DEV):
            copy(par, lax.rem(me + off, DEV), me).start()
        for off in range(1, DEV):
            copy(par, lax.rem(me + off, DEV), lax.rem(me + off, DEV)).wait_recv()
        total = gath_ref[par, 0]
        for d in range(1, DEV):
            total = total + gath_ref[par, d]
        v_ref[...] = q_ref[...] / total
        for off in range(1, DEV):
            copy(par, lax.rem(me + off, DEV), me).wait_send()
        return carry

    lax.fori_loop(0, SWEEPS, sweep, 0)


def plan_block(kern_ref, u_ref, v_ref, j):
    cols = pl.multiple_of(j * BLK, BLK)
    parts = []
    for h in range(BLK // LANES):
        vrow = v_ref[pl.ds(j * (BLK // LANES) + h, 1), :]
        parts.append(u_ref[...] * kern_ref[:, pl.ds(cols + h * LANES, LANES)] * vrow)
    return jnp.concatenate(parts, axis=1)


def gather_plan(at, chunks, plan_ref, send_sem, recv_sem, produce, near_end, column):
    def copy(owner, j, dest, kind):
        view = plan_ref.at[j, rows_of(owner), :]
        return pltpu.make_async_remote_copy(
            src_ref=view, dst_ref=view, send_sem=send_sem.at[kind, j],
            recv_sem=recv_sem.at[owner, j], device_id={"rows": dest})

    def send_own(j):
        copy(at.me, j, at.x0, 0).start()
        copy(at.me, j, at.y0, 1).start()
        copy(at.me, j, at.sib, 2).start()

    for j in range(AHEAD):
        produce(j)
        send_own(j)

    def turn(it, carry):
        @pl.when(it + AHEAD < chunks)
        def _():
            produce(it + AHEAD)
            send_own(it + AHEAD)

        @pl.when(it < chunks)
        def _():
            copy(at.x0, it, at.x0, 0).wait_recv()
            copy(at.x0, it, at.sib, 3).start()

            @pl.when(lax.rem(it, 2) == 0)
            def _():
                copy(at.x0, it, at.y0, 6).start()

            copy(at.y0, it, at.y0, 0).wait_recv()
            copy(at.y0, it, at.sib, 4).start()

            @pl.when(lax.rem(it, 2) == 1)
            def _():
                copy(at.y0, it, at.x0, 6).start()

        @pl.when(it == chunks - 1)
        def _():
            near_end()

        @pl.when((it >= LAG) & (it < LAG + chunks))
        def _():
            copy(at.d0, it - LAG, at.d0, 0).wait_recv()
            copy(at.d0, it - LAG, at.sib, 5).start()

        @pl.when(it >= LAG + 1)
        def _():
            j = it - LAG - 1
            for owner in (at.sib, at.x1, at.y1, at.d1):
                copy(owner, j, at.sib, 0).wait_recv()
            column(j)

        return carry

    lax.fori_loop(0, chunks + LAG + 1, turn, 0)

    def drain(j, carry):
        for kind in range(7):
            copy(at.me, j, at.sib, kind).wait_send()
        return carry

    lax.fori_loop(0, chunks, drain, 0)


def fgw_kernel(
    eps_ref, mass_ref, q_ref, src_hbm, tgt_hbm, plan_hbm, fsrc_hbm, ftgt_hbm, out_hbm,
    stage_ref, stage2_ref, feat_ref, plan_ref, tgt_ref, src_ref, fsrc_ref, a_ref, cross_ref, cost_ref, kern_ref,
    p_ref, u_ref, v_ref, part_ref, gath_ref,
    load_sem, plan_send, plan_recv, tgt_send, tgt_recv, sum_send, sum_recv,
):
    at = Place()
    me = at.me
    rows, cols = kern_ref.shape
    nblk = cols // BLK
    eps = eps_ref[0]

    def load_plan(j):
        return pltpu.make_async_copy(plan_hbm.at[:, pl.ds(pl.multiple_of(j * BLK, BLK), BLK)], stage_ref.at[j], load_sem.at[j])

    def load_tgt(j):
        return pltpu.make_async_copy(tgt_hbm.at[:, pl.ds(pl.multiple_of(j * BLK, BLK), BLK)], stage2_ref.at[j], load_sem.at[nblk + j])

    load_feat = pltpu.make_async_copy(ftgt_hbm, feat_ref.at[0], load_sem.at[2 * nblk])
    load_fsrc = pltpu.make_async_copy(fsrc_hbm, feat_ref.at[1], load_sem.at[2 * nblk + 1])
    load_src = pltpu.make_async_copy(src_hbm, cost_ref, load_sem.at[2 * nblk + 2])

    for j in range(nblk):
        load_plan(j).start()
    load_feat.start()
    load_fsrc.start()
    load_src.start()
    for j in range(nblk):
        load_tgt(j).start()

    barrier = pltpu.get_barrier_semaphore()
    for off in range(1, DEV):
        pl.semaphore_signal(barrier, inc=1, device_id={"rows": lax.rem(me + off, DEV)})

    eye = lax.broadcasted_iota(jnp.int32, (LANES, LANES), 0) == lax.broadcasted_iota(jnp.int32, (LANES, LANES), 1)
    for r in range(rows // LANES):
        line = jnp.broadcast_to(mass_ref[r:r + 1, :], (LANES, LANES))
        col = jnp.sum(jnp.where(eye, line, 0.0), axis=1, keepdims=True)
        p_ref[r * LANES:(r + 1) * LANES, :] = jnp.broadcast_to(col, (LANES, LANES))

    pl.semaphore_wait(barrier, DEV - 1)

    def cast_plan(j):
        if isinstance(j, int):
            load_plan(j).wait()
            plan_ref[j, rows_of(me), :] = stage_ref[j].astype(jnp.bfloat16)
            return

        @pl.when(j < nblk)
        def _():
            load_plan(j).wait()
            plan_ref[j, rows_of(me), :] = stage_ref[j].astype(jnp.bfloat16)

        @pl.when(j == nblk)
        def _():
            load_feat.wait()
            plan_ref[nblk, rows_of(me), :] = feat_ref[0].astype(jnp.bfloat16)

        @pl.when(j == AHEAD)
        def _():
            load_fsrc.wait()
            fsrc_ref[...] = feat_ref[1].astype(jnp.bfloat16)
            load_src.wait()
            src_ref[...] = cost_ref[...].astype(jnp.bfloat16)

        @pl.when(j < nblk)
        def _():
            load_tgt(j).wait()
            tgt_ref[j, rows_of(me), :] = stage2_ref[j].astype(jnp.bfloat16)

    def tcopy(owner, col, dest, kind):
        view = tgt_ref.at[col, rows_of(owner), :]
        return pltpu.make_async_remote_copy(
            src_ref=view, dst_ref=view, send_sem=tgt_send.at[kind, col],
            recv_sem=tgt_recv.at[owner, col], device_id={"rows": dest})

    out_x = (at.me, at.sib, at.y0, at.y1, at.d0)
    out_y = (at.sib, at.me, at.x0, at.x1, at.d1)
    in_x = (at.x0, at.x1, at.d0, at.d1, at.y0)
    in_y = (at.y1, at.y0, at.d0, at.d1, at.x1)

    def send_tgt():
        for j in range(AHEAD):
            load_tgt(j).wait()
            tgt_ref[j, rows_of(me), :] = stage2_ref[j].astype(jnp.bfloat16)
        for cx, cy in zip(out_x, out_y):
            tcopy(me, cx, at.x0, 0).start()
            tcopy(me, cy, at.y0, 1).start()

        def to_sib(j, carry):
            tcopy(me, j, at.sib, 2).start()
            return carry

        lax.fori_loop(0, nblk, to_sib, 0)

    def column(j):
        @pl.when(j < nblk)
        def _():
            prod = jnp.dot(src_ref[...], plan_ref[j], preferred_element_type=jnp.float32)
            a_ref[:, pl.ds(pl.multiple_of(j * BLK, BLK), BLK)] = prod.astype(jnp.bfloat16)

    gather_plan(at, nblk + 1, plan_ref, plan_send, plan_recv, cast_plan, send_tgt, column)

    def cross(j, carry):
        prod = lax.dot_general(
            fsrc_ref[...], plan_ref[nblk, rows_of(j), :], (((1,), (1,)), ((), ())), preferred_element_type=jnp.float32)
        cross_ref[:, pl.ds(pl.multiple_of(j * BLK, BLK), BLK)] = (-2.0 * ALPHA) * prod
        return carry

    lax.fori_loop(0, nblk, cross, 0)

    def mirror(owner, col):
        tgt_ref[owner, rows_of(col), :] = tgt_ref[col, rows_of(owner), :].T

    base = me - at.core
    xb, yb, db = at.x0 - at.core, at.y0 - at.core, at.d0 - at.core

    def mirror_own(t, carry):
        mirror(me, lax.rem(base + 2 + t, DEV))
        return carry

    lax.fori_loop(0, DEV - 2, mirror_own, 0)

    for k in range(5):
        tcopy(at.x0, in_x[k], at.x0, 0).wait_recv()
        tcopy(at.x0, in_x[k], at.sib, 3).start()
        if k == 1:
            tcopy(at.x0, at.x1, at.y0, 6).start()
        tcopy(at.y0, in_y[k], at.y0, 0).wait_recv()
        tcopy(at.y0, in_y[k], at.sib, 4).start()
        if k == 1:
            tcopy(at.y0, at.y0, at.x0, 6).start()
    for col in (at.d0, at.d1):
        tcopy(at.d0, col, at.d0, 0).wait_recv()
        tcopy(at.d0, col, at.sib, 5).start()

    def from_sib(j, carry):
        tcopy(at.sib, j, at.sib, 0).wait_recv()
        return carry

    lax.fori_loop(0, nblk, from_sib, 0)
    for col in (at.x1, at.x0, at.d1, at.d0, at.y1):
        tcopy(at.x1, col, at.sib, 0).wait_recv()
    for col in (at.y0, at.y1, at.d1, at.d0, at.x0):
        tcopy(at.y1, col, at.sib, 0).wait_recv()
    for col in (at.d1, at.d0):
        tcopy(at.d1, col, at.sib, 0).wait_recv()

    def mirror_sib(t, carry):
        mirror(at.sib, lax.rem(base + 2 + t, DEV))
        return carry

    lax.fori_loop(0, DEV - 2, mirror_sib, 0)

    def mirror_diag(t, carry):
        first = xb + (yb - xb) * (t // 4) + lax.rem(t // 2, 2)
        mirror(first, db + lax.rem(t, 2))
        return carry

    lax.fori_loop(0, 8, mirror_diag, 0)

    def mirror_xy(t, carry):
        mirror(xb + t, yb + t)
        mirror(yb + t, xb + 1 - t)
        return carry

    lax.fori_loop(0, 2, mirror_xy, 0)

    for cx, cy in zip(out_x, out_y):
        tcopy(me, cx, at.x0, 0).wait_send()
        tcopy(me, cy, at.y0, 1).wait_send()
    for k in range(5):
        tcopy(at.x0, in_x[k], at.sib, 3).wait_send()
        tcopy(at.y0, in_y[k], at.sib, 4).wait_send()
    for col in (at.d0, at.d1):
        tcopy(at.d0, col, at.sib, 5).wait_send()
    tcopy(at.x0, at.x1, at.y0, 6).wait_send()
    tcopy(at.y0, at.y0, at.x0, 6).wait_send()

    def sib_done(j, carry):
        tcopy(me, j, at.sib, 2).wait_send()
        return carry

    lax.fori_loop(0, nblk, sib_done, 0)

    def costs(j, carry):
        prod = jnp.dot(a_ref[...], tgt_ref[j], preferred_element_type=jnp.float32)
        where = pl.ds(pl.multiple_of(j * BLK, BLK), BLK)
        cost_ref[:, where] = cross_ref[:, where] - (2.0 * (1.0 - ALPHA)) * prod
        return carry

    def sweeps():
        lax.fori_loop(0, nblk, costs, 0)
        build_kernel(cost_ref, kern_ref, eps, rows, cols)
        sinkhorn(at, kern_ref, p_ref, q_ref, u_ref, v_ref, part_ref, gath_ref, sum_send, sum_recv, rows, cols)

    sweeps()

    def next_plan(j):
        plan_ref[j, rows_of(me), :] = plan_block(kern_ref, u_ref, v_ref, j).astype(jnp.bfloat16)

    gather_plan(at, nblk, plan_ref, plan_send, plan_recv, next_plan, lambda: None, column)
    sweeps()

    def store(j):
        return pltpu.make_async_copy(stage_ref.at[j], out_hbm.at[:, pl.ds(pl.multiple_of(j * BLK, BLK), BLK)], load_sem.at[j])

    def last_plan(j, carry):
        stage_ref[j] = plan_block(kern_ref, u_ref, v_ref, j)
        store(j).start()
        return carry

    lax.fori_loop(0, nblk, last_plan, 0)
    for j in range(nblk):
        store(j).wait()


def fgw(src, tgt, plan, mass, q, fsrc, ftgt, eps):
    rows, cols = plan.shape
    tiles = cols // LANES
    nblk = cols // BLK
    vmem = pl.BlockSpec(memory_space=pltpu.VMEM)
    hbm = pl.BlockSpec(memory_space=pl.ANY)
    f32, bf16 = jnp.float32, jnp.bfloat16
    return pl.pallas_call(
        fgw_kernel,
        out_shape=jax.ShapeDtypeStruct((rows, cols), f32),
        in_specs=[pl.BlockSpec(memory_space=pltpu.SMEM), vmem, vmem] + [hbm] * 5,
        out_specs=hbm,
        scratch_shapes=[
            pltpu.VMEM((nblk, BLK, BLK), f32),
            pltpu.VMEM((nblk, BLK, BLK), f32),
            pltpu.VMEM((2, BLK, BLK), f32),
            pltpu.VMEM((nblk + 1, DEV * BLK, BLK), bf16),
            pltpu.VMEM((nblk, DEV * BLK, BLK), bf16),
            pltpu.VMEM((rows, cols), bf16),
            pltpu.VMEM((BLK, BLK), bf16),
            pltpu.VMEM((rows, cols), bf16),
            pltpu.VMEM((rows, cols), f32),
            pltpu.VMEM((rows, cols), f32),
            pltpu.VMEM((rows, cols), f32),
            pltpu.VMEM((rows, LANES), f32),
            pltpu.VMEM((rows, LANES), f32),
            pltpu.VMEM((tiles, LANES), f32),
            pltpu.VMEM((2, tiles, LANES), f32),
            pltpu.VMEM((2, DEV, tiles, LANES), f32),
            pltpu.SemaphoreType.DMA((2 * nblk + 3,)),
            pltpu.SemaphoreType.DMA((7, nblk + 1)),
            pltpu.SemaphoreType.DMA((DEV, nblk + 1)),
            pltpu.SemaphoreType.DMA((7, nblk)),
            pltpu.SemaphoreType.DMA((DEV, nblk)),
            pltpu.SemaphoreType.DMA((2, DEV)),
            pltpu.SemaphoreType.DMA((2, DEV)),
        ],
        compiler_params=pltpu.CompilerParams(collective_id=0, has_side_effects=True, vmem_limit_bytes=60 << 20),
        name="fgw",
    )(eps, mass, q, src, tgt, plan, fsrc, ftgt)


def solution(mesh):
    def local_fgw(cost_src, cost_tgt, plan_init, mass_src, mass_tgt, feat_src, feat_tgt, epsilon):
        return fgw(
            cost_src, cost_tgt, plan_init, mass_src.reshape(-1, LANES), mass_tgt.reshape(-1, LANES),
            feat_src, feat_tgt, epsilon.reshape(1))

    row_spec = P(('pairs', 'rows'), None)
    vec_spec = P(('pairs', 'rows'))
    in_specs = (row_spec, row_spec, row_spec, vec_spec, P('pairs'), row_spec, row_spec, P())
    return jax.shard_map(local_fgw, mesh=mesh, in_specs=in_specs, out_specs=row_spec, check_vma=False)
```

time: 292 us -> 192 us (0.66)
  waiting for transfers between devices: 162 us -> 0 us
  Pallas kernels: 76.9 us -> 188 us
  matrix products: 30.2 us -> 0 us
  between operations: 13.9 us -> 0.66 us
  other arithmetic: 6.75 us -> 0 us
    all_gather x4 -> x0, waiting for transfers between devices: 162 us -> none  [the longest x2 98.7 us: local_fgw(): lax.all_gather(transport.astype(jnp.bfloat16), 'rows', tiled=True)]
    pallas_call x2 -> x1, Pallas kernels: 76.9 us -> 188 us  [fgw(): pl.pallas_call(fgw_kernel, out_shape=jax.ShapeDtypeStruct((rows, cols), f...]
    dot_general x3 -> x0, matrix products: 30.2 us -> none  [the longest x2 27.2 us: local_fgw(): jnp.dot(prod_a.astype(jnp.bfloat16), tgt_all, preferred_element_type=jnp....]
    convert_element_type x4 -> x0, other arithmetic: 6.75 us -> none  [the longest x1 2.88 us: local_fgw(): tgt_half = cost_tgt.astype(jnp.bfloat16)]
  transfers between devices with their start and end apart: 4 -> 0, of which waited for: 4 -> 0; matrix products, arithmetic and copies ran while one was open for 2% -> 0% of each run, Pallas kernels for 0% -> 0%
where the time goes in v2:
time: 192 us
  Pallas kernels  188 us (98%)
  local copies, waits for them, and re-layouts  3.14 us (2%)
    pallas_call x1, Pallas kernels, fgw(): pl.pallas_call(fgw_kernel, out_shape=jax.ShapeDtypeStruct((rows, cols), f...  188 us

profile of v2, /device:TPU:0, one launch (start us, length us, event | category | flops | bytes accessed | tf_op | source)
XLA Modules:
  0.0 191.7 jit_solution(13057229196481789383)
XLA Ops:
  0.7 187.9 %fgw.1 = f32[256,2048]{1,0:T(8,128)} custom-call(f32[1]{0:T(128)} %bitcast.3.eps_ref, f32[2,128]{1,0:T(2,128)} %bitcast.5, f32[16,128]{1,0:T(8,128)} %bitcast.4, f32[256,2048]{1,0:T(8,128)} %src_hbm.1, f32[256,2048]{1,0:T(8,128)} %tgt_hbm.1, f32[256,2048]{1,0:T(8,128)} %plan_hbm.1, f32[256,256]{1,0:T(8,128)} %fsrc_hbm.1, f32[256,256]{1,0:T(8,128)} %ftgt_hbm.1), custom_call_target="tpu_custom_call" | custom-call | tf_op jit(solution)/shard_map/fgw/pallas_call | solution.py:402
  188.6 3.1 %copy.11 = f32[256,2048]{1,0:T(8,128)} copy(f32[256,2048]{1,0:T(8,128)} %fgw.1) | data formatting | bytes 4194304

commit v3 on v2

--- a/solution.py
+++ b/solution.py
@@ -16,6 +16,7 @@
 DEV = 8
 AHEAD = 2
 LAG = 2
+EARLY = 7
 
 
 def tree_sum(vals):
@@ -42,83 +43,100 @@
         self.d0, self.d1 = self.me + dx + dy, self.sib + dx + dy
 
 
-def build_kernel(cost_ref, kern_ref, eps, rows, cols):
+def build_kernel(cost_ref, kern_ref, eps, start, rows, cols):
     tiles = cols // LANES
 
     def block(b, carry):
-        row = pl.multiple_of(b * SUB, SUB)
+        row = pl.multiple_of(start + b * SUB, SUB)
         vals = [cost_ref[pl.ds(row, SUB), t * LANES:(t + 1) * LANES] for t in range(tiles)]
         low = functools.reduce(jnp.minimum, vals)
         low = jnp.min(low, axis=1, keepdims=True)
         for t in range(tiles):
-            kern_ref[pl.ds(row, SUB), t * LANES:(t + 1) * LANES] = jnp.exp((low - vals[t]) / eps)
+            kern_ref[0, pl.ds(row, SUB), t * LANES:(t + 1) * LANES] = jnp.exp((low - vals[t]) / eps)
         return carry
 
     lax.fori_loop(0, rows // SUB, block, 0, unroll=4)
 
 
-def sinkhorn(at, kern_ref, p_ref, q_ref, u_ref, v_ref, part_ref, gath_ref, send_sem, recv_sem, rows, cols):
+def spread(line, eye):
+    wide = jnp.broadcast_to(line, (LANES, LANES))
+    col = jnp.sum(jnp.where(eye, wide, 0.0), axis=1, keepdims=True)
+    return jnp.broadcast_to(col, (LANES, LANES))
+
+
+def sinkhorn(at, kern_ref, p_ref, q_ref, u_ref, v_ref, part_ref, gath_ref, send_sem, recv_sem):
+    halves, rows, cols = kern_ref.shape
     tiles = cols // LANES
-    blocks = rows // SUB
-    me = at.me
-
-    def copy(par, peer, slot):
+    blocks = [(h, b) for h in range(halves) for b in range(rows // SUB)]
+    chip = at.me // 2
+    peers = (at.x0, at.y0, at.d0)
+
+    def copy(par, k, slot):
         return pltpu.make_async_remote_copy(
             src_ref=part_ref.at[par], dst_ref=gath_ref.at[par, slot],
-            send_sem=send_sem.at[par, peer], recv_sem=recv_sem.at[par, slot], device_id={"rows": peer})
+            send_sem=send_sem.at[par, k], recv_sem=recv_sem.at[par, slot], device_id={"rows": peers[k]})
 
     v_ref[...] = jnp.ones_like(v_ref)
 
     def sweep(step, carry):
         par = lax.rem(step, 2)
         vrow = [jnp.broadcast_to(v_ref[t:t + 1, :], (SUB, LANES)) for t in range(tiles)]
-        for b in range(blocks):
-            prods = [kern_ref[b * SUB:(b + 1) * SUB, t * LANES:(t + 1) * LANES] * vrow[t] for t in range(tiles)]
+        for h, b in blocks:
+            prods = [kern_ref[h, b * SUB:(b + 1) * SUB, t * LANES:(t + 1) * LANES] * vrow[t] for t in range(tiles)]
             dots = jnp.sum(tree_sum(prods), axis=1, keepdims=True)
-            u_ref[b * SUB:(b + 1) * SUB, :] = p_ref[b * SUB:(b + 1) * SUB, :] / dots
+            at_row = slice(h * rows + b * SUB, h * rows + (b + 1) * SUB)
+            u_ref[at_row, :] = p_ref[at_row, :] / dots
         acc = [None] * tiles
-        for b in range(blocks):
-            scale = u_ref[b * SUB:(b + 1) * SUB, :]
+        for h, b in blocks:
+            scale = u_ref[h * rows + b * SUB:h * rows + (b + 1) * SUB, :]
             for t in range(tiles):
-                term = kern_ref[b * SUB:(b + 1) * SUB, t * LANES:(t + 1) * LANES] * scale
+                term = kern_ref[h, b * SUB:(b + 1) * SUB, t * LANES:(t + 1) * LANES] * scale
                 acc[t] = term if acc[t] is None else acc[t] + term
         sums = jnp.concatenate([jnp.sum(a, axis=0, keepdims=True) for a in acc], axis=0)
         part_ref[par] = sums
-        gath_ref[par, me] = sums
-        for off in range(1, DEV):
-            copy(par, lax.rem(me + off, DEV), me).start()
-        for off in range(1, DEV):
-            copy(par, lax.rem(me + off, DEV), lax.rem(me + off, DEV)).wait_recv()
+        for k in (2, 0, 1):
+            copy(par, k, chip).start()
+        gath_ref[par, chip] = sums
+        for k in range(3):
+            copy(par, k, peers[k] // 2).wait_recv()
         total = gath_ref[par, 0]
-        for d in range(1, DEV):
+        for d in range(1, DEV // 2):
             total = total + gath_ref[par, d]
         v_ref[...] = q_ref[...] / total
-        for off in range(1, DEV):
-            copy(par, lax.rem(me + off, DEV), me).wait_send()
+        for k in range(3):
+            copy(par, k, chip).wait_send()
         return carry
 
     lax.fori_loop(0, SWEEPS, sweep, 0)
 
 
-def plan_block(kern_ref, u_ref, v_ref, j):
-    cols = pl.multiple_of(j * BLK, BLK)
+def plan_block(kern, scale, v_ref, j):
     parts = []
     for h in range(BLK // LANES):
         vrow = v_ref[pl.ds(j * (BLK // LANES) + h, 1), :]
-        parts.append(u_ref[...] * kern_ref[:, pl.ds(cols + h * LANES, LANES)] * vrow)
+        parts.append(scale * kern(h) * vrow)
     return jnp.concatenate(parts, axis=1)
 
 
-def gather_plan(at, chunks, plan_ref, send_sem, recv_sem, produce, near_end, column):
+def gather_plan(at, chunks, plan_ref, send_sem, recv_sem, produce, near_end, column, form=None):
     def copy(owner, j, dest, kind):
         view = plan_ref.at[j, rows_of(owner), :]
         return pltpu.make_async_remote_copy(
             src_ref=view, dst_ref=view, send_sem=send_sem.at[kind, j],
             recv_sem=recv_sem.at[owner, j], device_id={"rows": dest})
 
+    def over_links(j):
+        return True if form is None else (at.core == 1) | (j >= EARLY)
+
+    def when(cond):
+        return (lambda f: f()) if cond is True else pl.when(cond)
+
     def send_own(j):
-        copy(at.me, j, at.x0, 0).start()
-        copy(at.me, j, at.y0, 1).start()
+        @when(over_links(j))
+        def _():
+            copy(at.me, j, at.x0, 0).start()
+            copy(at.me, j, at.y0, 1).start()
+
         copy(at.me, j, at.sib, 2).start()
 
     for j in range(AHEAD):
@@ -131,7 +149,7 @@
             produce(it + AHEAD)
             send_own(it + AHEAD)
 
-        @pl.when(it < chunks)
+        @pl.when((it < chunks) & over_links(it))
         def _():
             copy(at.x0, it, at.x0, 0).wait_recv()
             copy(at.x0, it, at.sib, 3).start()
@@ -147,11 +165,18 @@
             def _():
                 copy(at.y0, it, at.x0, 6).start()
 
+        if form is not None:
+            @pl.when((it < chunks) & (at.core == 0) & (it < EARLY))
+            def _():
+                for k, owner in enumerate((at.x0, at.y0, at.d0)):
+                    plan_ref[it, rows_of(owner), :] = form(k, it).astype(jnp.bfloat16)
+                    copy(owner, it, at.sib, 3 + k).start()
+
         @pl.when(it == chunks - 1)
         def _():
             near_end()
 
-        @pl.when((it >= LAG) & (it < LAG + chunks))
+        @pl.when((it >= LAG) & (it < LAG + chunks) & over_links(it - LAG))
         def _():
             copy(at.d0, it - LAG, at.d0, 0).wait_recv()
             copy(at.d0, it - LAG, at.sib, 5).start()
@@ -168,8 +193,14 @@
     lax.fori_loop(0, chunks + LAG + 1, turn, 0)
 
     def drain(j, carry):
-        for kind in range(7):
+        for kind in (2, 3, 4, 5):
             copy(at.me, j, at.sib, kind).wait_send()
+
+        @when(over_links(j))
+        def _():
+            for kind in (0, 1, 6):
+                copy(at.me, j, at.sib, kind).wait_send()
+
         return carry
 
     lax.fori_loop(0, chunks, drain, 0)
@@ -178,12 +209,13 @@
 def fgw_kernel(
     eps_ref, mass_ref, q_ref, src_hbm, tgt_hbm, plan_hbm, fsrc_hbm, ftgt_hbm, out_hbm,
     stage_ref, stage2_ref, feat_ref, plan_ref, tgt_ref, src_ref, fsrc_ref, a_ref, cross_ref, cost_ref, kern_ref,
-    p_ref, u_ref, v_ref, part_ref, gath_ref,
-    load_sem, plan_send, plan_recv, tgt_send, tgt_recv, sum_send, sum_recv,
+    early_ref, p_ref, u_ref, v_ref, other_ref, part_ref, gath_ref, msg_ref, news_ref, mass2_ref,
+    load_sem, plan_send, plan_recv, tgt_send, tgt_recv, sum_send, sum_recv, half_send, half_recv,
+    early_send, early_recv, msg_send, msg_recv,
 ):
     at = Place()
     me = at.me
-    rows, cols = kern_ref.shape
+    _, rows, cols = kern_ref.shape
     nblk = cols // BLK
     eps = eps_ref[0]
 
@@ -209,13 +241,12 @@
     for off in range(1, DEV):
         pl.semaphore_signal(barrier, inc=1, device_id={"rows": lax.rem(me + off, DEV)})
 
+    pl.semaphore_wait(barrier, DEV - 1)
+
+    swap = pltpu.make_async_remote_copy(
+        src_ref=mass_ref, dst_ref=mass2_ref, send_sem=half_send.at[4], recv_sem=half_recv.at[4], device_id={"rows": at.sib})
+    swap.start()
     eye = lax.broadcasted_iota(jnp.int32, (LANES, LANES), 0) == lax.broadcasted_iota(jnp.int32, (LANES, LANES), 1)
-    for r in range(rows // LANES):
-        line = jnp.broadcast_to(mass_ref[r:r + 1, :], (LANES, LANES))
-        col = jnp.sum(jnp.where(eye, line, 0.0), axis=1, keepdims=True)
-        p_ref[r * LANES:(r + 1) * LANES, :] = jnp.broadcast_to(col, (LANES, LANES))
-
-    pl.semaphore_wait(barrier, DEV - 1)
 
     def cast_plan(j):
         if isinstance(j, int):
@@ -277,6 +308,11 @@
             a_ref[:, pl.ds(pl.multiple_of(j * BLK, BLK), BLK)] = prod.astype(jnp.bfloat16)
 
     gather_plan(at, nblk + 1, plan_ref, plan_send, plan_recv, cast_plan, send_tgt, column)
+
+    swap.wait()
+    for r in range(rows // LANES):
+        p_ref[r * LANES:(r + 1) * LANES, :] = spread(mass_ref[r:r + 1, :], eye)
+        p_ref[rows + r * LANES:rows + (r + 1) * LANES, :] = spread(mass2_ref[r:r + 1, :], eye)
 
     def cross(j, carry):
         prod = lax.dot_general(
@@ -366,24 +402,124 @@
         cost_ref[:, where] = cross_ref[:, where] - (2.0 * (1.0 - ALPHA)) * prod
         return carry
 
-    def sweeps():
+    def half(i):
+        part = pl.ds(i * (rows // 4), rows // 4)
+        return pltpu.make_async_remote_copy(
+            src_ref=kern_ref.at[0, part], dst_ref=kern_ref.at[1, part], send_sem=half_send.at[i],
+            recv_sem=half_recv.at[i], device_id={"rows": at.sib})
+
+    def early(src, j, slot, dest, kind):
+        return pltpu.make_async_remote_copy(
+            src_ref=src, dst_ref=early_ref.at[slot, j], send_sem=early_send.at[kind, j],
+            recv_sem=early_recv.at[slot, j], device_id={"rows": dest})
+
+    def own_part(j):
+        return kern_ref.at[0, :, pl.ds(pl.multiple_of(j * BLK, BLK), BLK)]
+
+    def early_round():
+        def send(j):
+            early(own_part(j), j, 0, at.x0, 0).start()
+            early(own_part(j), j, 1, at.y0, 1).start()
+
+        for j in range(AHEAD):
+            send(j)
+
+        def turn(j, carry):
+            @pl.when(j + AHEAD < EARLY)
+            def _():
+                send(j + AHEAD)
+
+            early(own_part(j), j, 0, at.x0, 0).wait_recv()
+
+            @pl.when(lax.rem(j, 2) == 0)
+            def _():
+                early(early_ref.at[0, j], j, 2, at.y0, 2).start()
+
+            early(own_part(j), j, 1, at.y0, 1).wait_recv()
+
+            @pl.when(lax.rem(j, 2) == 1)
+            def _():
+                early(early_ref.at[1, j], j, 2, at.x0, 2).start()
+
+            return carry
+
+        lax.fori_loop(0, EARLY, turn, 0)
+
+        def done(j, carry):
+            early(own_part(j), j, 2, at.x0, 2).wait_recv()
+            for kind in range(3):
+                early(own_part(j), j, kind, at.x0, kind).wait_send()
+            return carry
+
+        lax.fori_loop(0, EARLY, done, 0)
+
+    tiles = cols // LANES
+    across = (at.sib, at.x1, at.y1, at.d1)
+
+    def news(k):
+        return pltpu.make_async_remote_copy(
+            src_ref=msg_ref, dst_ref=news_ref.at[k], send_sem=msg_send.at[k], recv_sem=msg_recv.at[k],
+            device_id={"rows": across[k]})
+
+    def sweeps(first):
+        reach = len(across) if first else 1
         lax.fori_loop(0, nblk, costs, 0)
-        build_kernel(cost_ref, kern_ref, eps, rows, cols)
-        sinkhorn(at, kern_ref, p_ref, q_ref, u_ref, v_ref, part_ref, gath_ref, sum_send, sum_recv, rows, cols)
-
-    sweeps()
+        for i in range(4):
+            build_kernel(cost_ref, kern_ref, eps, i * (rows // 4), rows // 4, cols)
+
+            @pl.when(at.core == 0)
+            def _():
+                half(i).start()
+
+        @pl.when(at.core == 1)
+        def _():
+            for i in range(4):
+                half(i).wait_recv()
+            sinkhorn(at, kern_ref, p_ref, q_ref, u_ref, v_ref, part_ref, gath_ref, sum_send, sum_recv)
+            msg_ref[:tiles] = v_ref[...]
+            msg_ref[tiles:] = jnp.zeros_like(msg_ref[tiles:])
+            for r in range(rows // LANES):
+                scale = u_ref[rows + r * LANES:rows + (r + 1) * LANES, :]
+                msg_ref[tiles + r:tiles + r + 1] = jnp.sum(jnp.where(eye, scale, 0.0), axis=0, keepdims=True)
+            for k in range(reach):
+                news(k).start()
+            for k in range(reach):
+                news(k).wait_send()
+
+        @pl.when(at.core == 0)
+        def _():
+            if first:
+                early_round()
+            for i in range(4):
+                half(i).wait_send()
+            for k in range(reach):
+                news(k).wait_recv()
+            v_ref[...] = news_ref[0, :tiles]
+            for r in range(rows // LANES):
+                u_ref[r * LANES:(r + 1) * LANES, :] = spread(news_ref[0, tiles + r:tiles + r + 1], eye)
+                for k in range(1, reach):
+                    other_ref[k - 1, r * LANES:(r + 1) * LANES, :] = spread(news_ref[k, tiles + r:tiles + r + 1], eye)
+
+    def own_block(j):
+        cols_at = pl.multiple_of(j * BLK, BLK)
+        return plan_block(lambda h: kern_ref[0, :, pl.ds(cols_at + h * LANES, LANES)], u_ref[:rows, :], v_ref, j)
+
+    sweeps(True)
 
     def next_plan(j):
-        plan_ref[j, rows_of(me), :] = plan_block(kern_ref, u_ref, v_ref, j).astype(jnp.bfloat16)
-
-    gather_plan(at, nblk, plan_ref, plan_send, plan_recv, next_plan, lambda: None, column)
-    sweeps()
+        plan_ref[j, rows_of(me), :] = own_block(j).astype(jnp.bfloat16)
+
+    def form(k, j):
+        return plan_block(lambda h: early_ref[k, j, :, h * LANES:(h + 1) * LANES], other_ref[k], v_ref, j)
+
+    gather_plan(at, nblk, plan_ref, plan_send, plan_recv, next_plan, lambda: None, column, form)
+    sweeps(False)
 
     def store(j):
         return pltpu.make_async_copy(stage_ref.at[j], out_hbm.at[:, pl.ds(pl.multiple_of(j * BLK, BLK), BLK)], load_sem.at[j])
 
     def last_plan(j, carry):
-        stage_ref[j] = plan_block(kern_ref, u_ref, v_ref, j)
+        stage_ref[j] = own_block(j)
         store(j).start()
         return carry
 
@@ -415,19 +551,30 @@
             pltpu.VMEM((rows, cols), bf16),
             pltpu.VMEM((rows, cols), f32),
             pltpu.VMEM((rows, cols), f32),
-            pltpu.VMEM((rows, cols), f32),
-            pltpu.VMEM((rows, LANES), f32),
-            pltpu.VMEM((rows, LANES), f32),
+            pltpu.VMEM((2, rows, cols), f32),
+            pltpu.VMEM((3, EARLY, BLK, BLK), f32),
+            pltpu.VMEM((2 * rows, LANES), f32),
+            pltpu.VMEM((2 * rows, LANES), f32),
             pltpu.VMEM((tiles, LANES), f32),
+            pltpu.VMEM((3, rows, LANES), f32),
             pltpu.VMEM((2, tiles, LANES), f32),
-            pltpu.VMEM((2, DEV, tiles, LANES), f32),
+            pltpu.VMEM((2, DEV // 2, tiles, LANES), f32),
+            pltpu.VMEM((tiles + SUB, LANES), f32),
+            pltpu.VMEM((4, tiles + SUB, LANES), f32),
+            pltpu.VMEM((rows // LANES, LANES), f32),
             pltpu.SemaphoreType.DMA((2 * nblk + 3,)),
             pltpu.SemaphoreType.DMA((7, nblk + 1)),
             pltpu.SemaphoreType.DMA((DEV, nblk + 1)),
             pltpu.SemaphoreType.DMA((7, nblk)),
             pltpu.SemaphoreType.DMA((DEV, nblk)),
-            pltpu.SemaphoreType.DMA((2, DEV)),
-            pltpu.SemaphoreType.DMA((2, DEV)),
+            pltpu.SemaphoreType.DMA((2, 3)),
+            pltpu.SemaphoreType.DMA((2, DEV // 2)),
+            pltpu.SemaphoreType.DMA((5,)),
+            pltpu.SemaphoreType.DMA((5,)),
+            pltpu.SemaphoreType.DMA((3, EARLY)),
+            pltpu.SemaphoreType.DMA((3, EARLY)),
+            pltpu.SemaphoreType.DMA((4,)),
+            pltpu.SemaphoreType.DMA((4,)),
         ],
         compiler_params=pltpu.CompilerParams(collective_id=0, has_side_effects=True, vmem_limit_bytes=60 << 20),
         name="fgw",

time: 192 us -> 172 us (0.90)
  Pallas kernels: 188 us -> 168 us
    pallas_call x1, Pallas kernels: 188 us -> 168 us  [fgw(): pl.pallas_call(fgw_kernel, out_shape=jax.ShapeDtypeStruct((rows, cols), f...]
where the time goes in v3:
time: 172 us
  Pallas kernels  168 us (98%)
  local copies, waits for them, and re-layouts  3.14 us (2%)
    pallas_call x1, Pallas kernels, fgw(): pl.pallas_call(fgw_kernel, out_shape=jax.ShapeDtypeStruct((rows, cols), f...  168 us

profile of v3, /device:TPU:0, one launch (start us, length us, event | category | flops | bytes accessed | tf_op | source)
XLA Modules:
  0.0 172.1 jit_solution(15760650874873933586)
XLA Ops:
  0.7 168.3 %fgw.1 = f32[256,2048]{1,0:T(8,128)} custom-call(f32[1]{0:T(128)} %bitcast.3.eps_ref, f32[2,128]{1,0:T(2,128)} %bitcast.5, f32[16,128]{1,0:T(8,128)} %bitcast.4, f32[256,2048]{1,0:T(8,128)} %src_hbm.1, f32[256,2048]{1,0:T(8,128)} %tgt_hbm.1, f32[256,2048]{1,0:T(8,128)} %plan_hbm.1, f32[256,256]{1,0:T(8,128)} %fsrc_hbm.1, f32[256,256]{1,0:T(8,128)} %ftgt_hbm.1), custom_call_target="tpu_custom_call" | custom-call | tf_op jit(solution)/shard_map/fgw/pallas_call | solution.py:538
  169.0 3.1 %copy.11 = f32[256,2048]{1,0:T(8,128)} copy(f32[256,2048]{1,0:T(8,128)} %fgw.1) | data formatting | bytes 4194304

commit v4 on v3

--- a/solution.py
+++ b/solution.py
@@ -43,16 +43,18 @@
         self.d0, self.d1 = self.me + dx + dy, self.sib + dx + dy
 
 
-def build_kernel(cost_ref, kern_ref, eps, start, rows, cols):
+def build_kernel(cost_ref, kern_ref, eps, half, rows, cols):
     tiles = cols // LANES
+    inv_eps = 1.0 / jnp.full((SUB, LANES), eps, jnp.float32)
 
     def block(b, carry):
-        row = pl.multiple_of(start + b * SUB, SUB)
-        vals = [cost_ref[pl.ds(row, SUB), t * LANES:(t + 1) * LANES] for t in range(tiles)]
+        row = pl.multiple_of(b * SUB, SUB)
+        at_row = pl.ds(half * rows + row, SUB)
+        vals = [cost_ref[at_row, t * LANES:(t + 1) * LANES] for t in range(tiles)]
         low = functools.reduce(jnp.minimum, vals)
         low = jnp.min(low, axis=1, keepdims=True)
         for t in range(tiles):
-            kern_ref[0, pl.ds(row, SUB), t * LANES:(t + 1) * LANES] = jnp.exp((low - vals[t]) / eps)
+            kern_ref[half, pl.ds(row, SUB), t * LANES:(t + 1) * LANES] = jnp.exp((low - vals[t]) * inv_eps)
         return carry
 
     lax.fori_loop(0, rows // SUB, block, 0, unroll=4)
@@ -207,10 +209,10 @@
 
 
 def fgw_kernel(
-    eps_ref, mass_ref, q_ref, src_hbm, tgt_hbm, plan_hbm, fsrc_hbm, ftgt_hbm, out_hbm,
+    eps_ref, mass_ref, q_ref, src_hbm, tgt_hbm, plan_hbm, fsrc_hbm, ftgt_hbm, out_ref,
     stage_ref, stage2_ref, feat_ref, plan_ref, tgt_ref, src_ref, fsrc_ref, a_ref, cross_ref, cost_ref, kern_ref,
     early_ref, p_ref, u_ref, v_ref, other_ref, part_ref, gath_ref, msg_ref, news_ref, mass2_ref,
-    load_sem, plan_send, plan_recv, tgt_send, tgt_recv, sum_send, sum_recv, half_send, half_recv,
+    load_sem, plan_send, plan_recv, tgt_send, tgt_recv, sum_send, sum_recv, a_send, a_recv, swap_send, swap_recv,
     early_send, early_recv, msg_send, msg_recv,
 ):
     at = Place()
@@ -227,7 +229,7 @@
 
     load_feat = pltpu.make_async_copy(ftgt_hbm, feat_ref.at[0], load_sem.at[2 * nblk])
     load_fsrc = pltpu.make_async_copy(fsrc_hbm, feat_ref.at[1], load_sem.at[2 * nblk + 1])
-    load_src = pltpu.make_async_copy(src_hbm, cost_ref, load_sem.at[2 * nblk + 2])
+    load_src = pltpu.make_async_copy(src_hbm, cost_ref.at[:rows], load_sem.at[2 * nblk + 2])
 
     for j in range(nblk):
         load_plan(j).start()
@@ -244,8 +246,11 @@
     pl.semaphore_wait(barrier, DEV - 1)
 
     swap = pltpu.make_async_remote_copy(
-        src_ref=mass_ref, dst_ref=mass2_ref, send_sem=half_send.at[4], recv_sem=half_recv.at[4], device_id={"rows": at.sib})
+        src_ref=mass_ref, dst_ref=mass2_ref, send_sem=swap_send.at[0], recv_sem=swap_recv.at[0], device_id={"rows": at.sib})
     swap.start()
+    swap_feat = pltpu.make_async_remote_copy(
+        src_ref=fsrc_ref.at[:BLK], dst_ref=fsrc_ref.at[BLK:], send_sem=swap_send.at[1], recv_sem=swap_recv.at[1],
+        device_id={"rows": at.sib})
     eye = lax.broadcasted_iota(jnp.int32, (LANES, LANES), 0) == lax.broadcasted_iota(jnp.int32, (LANES, LANES), 1)
 
     def cast_plan(j):
@@ -267,9 +272,10 @@
         @pl.when(j == AHEAD)
         def _():
             load_fsrc.wait()
-            fsrc_ref[...] = feat_ref[1].astype(jnp.bfloat16)
+            fsrc_ref[:BLK] = feat_ref[1].astype(jnp.bfloat16)
+            swap_feat.start()
             load_src.wait()
-            src_ref[...] = cost_ref[...].astype(jnp.bfloat16)
+            src_ref[...] = cost_ref[:rows, :].astype(jnp.bfloat16)
 
         @pl.when(j < nblk)
         def _():
@@ -283,9 +289,9 @@
             recv_sem=tgt_recv.at[owner, col], device_id={"rows": dest})
 
     out_x = (at.me, at.sib, at.y0, at.y1, at.d0)
-    out_y = (at.sib, at.me, at.x0, at.x1, at.d1)
+    out_y = (at.me, at.sib, at.x0, at.x1, at.d1)
     in_x = (at.x0, at.x1, at.d0, at.d1, at.y0)
-    in_y = (at.y1, at.y0, at.d0, at.d1, at.x1)
+    in_y = (at.y0, at.y1, at.d0, at.d1, at.x1)
 
     def send_tgt():
         for j in range(AHEAD):
@@ -301,83 +307,163 @@
 
         lax.fori_loop(0, nblk, to_sib, 0)
 
-    def column(j):
+    def a_copy(j):
+        cols_at = pl.ds(pl.multiple_of(j * BLK, BLK), BLK)
+        return pltpu.make_async_remote_copy(
+            src_ref=a_ref.at[:rows, cols_at], dst_ref=a_ref.at[rows:, cols_at], send_sem=a_send.at[j],
+            recv_sem=a_recv.at[j], device_id={"rows": at.sib})
+
+    def make_column(j):
+        prod = jnp.dot(src_ref[...], plan_ref[j], preferred_element_type=jnp.float32)
+        a_ref[:rows, pl.ds(pl.multiple_of(j * BLK, BLK), BLK)] = prod.astype(jnp.bfloat16)
+
+        @pl.when(at.core == 0)
+        def _():
+            a_copy(j).start()
+
+    def first_column(j):
         @pl.when(j < nblk)
         def _():
-            prod = jnp.dot(src_ref[...], plan_ref[j], preferred_element_type=jnp.float32)
-            a_ref[:, pl.ds(pl.multiple_of(j * BLK, BLK), BLK)] = prod.astype(jnp.bfloat16)
-
-    gather_plan(at, nblk + 1, plan_ref, plan_send, plan_recv, cast_plan, send_tgt, column)
+            make_column(j)
+
+    gather_plan(at, nblk + 1, plan_ref, plan_send, plan_recv, cast_plan, send_tgt, first_column)
+
+    def on_reach(f):
+        @pl.when(at.core == 1)
+        def _():
+            f(2 * rows)
+
+        @pl.when(at.core == 0)
+        def _():
+            f(rows)
 
     swap.wait()
+    swap_feat.wait()
     for r in range(rows // LANES):
         p_ref[r * LANES:(r + 1) * LANES, :] = spread(mass_ref[r:r + 1, :], eye)
         p_ref[rows + r * LANES:rows + (r + 1) * LANES, :] = spread(mass2_ref[r:r + 1, :], eye)
 
-    def cross(j, carry):
-        prod = lax.dot_general(
-            fsrc_ref[...], plan_ref[nblk, rows_of(j), :], (((1,), (1,)), ((), ())), preferred_element_type=jnp.float32)
-        cross_ref[:, pl.ds(pl.multiple_of(j * BLK, BLK), BLK)] = (-2.0 * ALPHA) * prod
-        return carry
-
-    lax.fori_loop(0, nblk, cross, 0)
+    def crosses(reach):
+        def cross(j, carry):
+            prod = lax.dot_general(
+                fsrc_ref[:reach, :], plan_ref[nblk, rows_of(j), :], (((1,), (1,)), ((), ())),
+                preferred_element_type=jnp.float32)
+            where = pl.ds(pl.multiple_of(j * BLK, BLK), BLK)
+            cross_ref[:reach, where] = (-2.0 * ALPHA) * prod
+            cost_ref[:reach, where] = (-2.0 * ALPHA) * prod
+            return carry
+
+        lax.fori_loop(0, nblk, cross, 0)
+
+    on_reach(crosses)
+
+    @pl.when(at.core == 1)
+    def _():
+        def arrived(j, carry):
+            a_copy(j).wait_recv()
+            return carry
+
+        lax.fori_loop(0, nblk, arrived, 0)
+
+    def term(reach, i, col):
+        lhs = a_ref[:reach, pl.ds(pl.multiple_of(i * BLK, BLK), BLK)]
+        prod = jnp.dot(lhs, tgt_ref[col, rows_of(i), :], preferred_element_type=jnp.float32)
+        return (2.0 * (1.0 - ALPHA)) * prod
+
+    def add(i, col):
+        def go(reach):
+            where = pl.ds(pl.multiple_of(col * BLK, BLK), BLK)
+            cost_ref[:reach, where] = cost_ref[:reach, where] - term(reach, i, col)
+
+        on_reach(go)
 
     def mirror(owner, col):
         tgt_ref[owner, rows_of(col), :] = tgt_ref[col, rows_of(owner), :].T
 
+    def use(owner, col, paired):
+        add(owner, col)
+
+        @pl.when(paired)
+        def _():
+            mirror(owner, col)
+            add(col, owner)
+
     base = me - at.core
-    xb, yb, db = at.x0 - at.core, at.y0 - at.core, at.d0 - at.core
-
-    def mirror_own(t, carry):
-        mirror(me, lax.rem(base + 2 + t, DEV))
+
+    def use_row(owner):
+        def body(t, carry):
+            use(owner, lax.rem(base + t, DEV), t >= 2)
+            return carry
+
+        lax.fori_loop(0, DEV, body, 0)
+
+    use_row(me)
+
+    def stream(k, s, other):
+        core = lax.rem(at.core + other, 2)
+        xb, yb, db = at.x0 - at.core, at.y0 - at.core, at.d0 - at.core
+        near = xb + s * (yb - xb)
+        far = yb + s * (xb - yb)
+        which = k // 2
+        chip = jnp.where(which == 0, near, jnp.where(which == 1, db, far))
+        flip = jnp.where(which == 2, s, 0)
+        return near + core, chip + lax.rem(core + k + flip, 2)
+
+    def arrivals(k, carry):
+        for s, fwd in ((0, 3), (1, 4)):
+            owner, col = stream(k, s, 0)
+            tcopy(owner, col, at.sib, 0).wait_recv()
+            tcopy(owner, col, at.sib, fwd).start()
+            if s == 0:
+                @pl.when(k == 1)
+                def _():
+                    tcopy(at.x0, at.x1, at.y0, 6).start()
+            else:
+                @pl.when(k == 0)
+                def _():
+                    tcopy(at.y0, at.y0, at.x0, 6).start()
+
+        @pl.when(k == 0)
+        def _():
+            def from_sib(j, c):
+                tcopy(at.sib, j, at.sib, 0).wait_recv()
+                return c
+
+            lax.fori_loop(0, nblk, from_sib, 0)
+            use_row(at.sib)
+
+        def near(s, c):
+            use(*stream(k, s, 0), k >= 2)
+            return c
+
+        lax.fori_loop(0, 2, near, 0)
+
+        def near_other(s, c):
+            owner, col = stream(k, s, 1)
+            tcopy(owner, col, at.sib, 0).wait_recv()
+            use(owner, col, k >= 2)
+            return c
+
+        lax.fori_loop(0, 2, near_other, 0)
         return carry
 
-    lax.fori_loop(0, DEV - 2, mirror_own, 0)
-
-    for k in range(5):
-        tcopy(at.x0, in_x[k], at.x0, 0).wait_recv()
-        tcopy(at.x0, in_x[k], at.sib, 3).start()
-        if k == 1:
-            tcopy(at.x0, at.x1, at.y0, 6).start()
-        tcopy(at.y0, in_y[k], at.y0, 0).wait_recv()
-        tcopy(at.y0, in_y[k], at.sib, 4).start()
-        if k == 1:
-            tcopy(at.y0, at.y0, at.x0, 6).start()
+    lax.fori_loop(0, 5, arrivals, 0)
     for col in (at.d0, at.d1):
         tcopy(at.d0, col, at.d0, 0).wait_recv()
         tcopy(at.d0, col, at.sib, 5).start()
 
-    def from_sib(j, carry):
-        tcopy(at.sib, j, at.sib, 0).wait_recv()
+    def diag(t, carry):
+        owner = at.d0 + (t // 2) * (at.d1 - at.d0)
+        col = at.d0 + lax.rem(t, 2) * (at.d1 - at.d0)
+
+        @pl.when(t >= 2)
+        def _():
+            tcopy(owner, col, at.sib, 0).wait_recv()
+
+        add(owner, col)
         return carry
 
-    lax.fori_loop(0, nblk, from_sib, 0)
-    for col in (at.x1, at.x0, at.d1, at.d0, at.y1):
-        tcopy(at.x1, col, at.sib, 0).wait_recv()
-    for col in (at.y0, at.y1, at.d1, at.d0, at.x0):
-        tcopy(at.y1, col, at.sib, 0).wait_recv()
-    for col in (at.d1, at.d0):
-        tcopy(at.d1, col, at.sib, 0).wait_recv()
-
-    def mirror_sib(t, carry):
-        mirror(at.sib, lax.rem(base + 2 + t, DEV))
-        return carry
-
-    lax.fori_loop(0, DEV - 2, mirror_sib, 0)
-
-    def mirror_diag(t, carry):
-        first = xb + (yb - xb) * (t // 4) + lax.rem(t // 2, 2)
-        mirror(first, db + lax.rem(t, 2))
-        return carry
-
-    lax.fori_loop(0, 8, mirror_diag, 0)
-
-    def mirror_xy(t, carry):
-        mirror(xb + t, yb + t)
-        mirror(yb + t, xb + 1 - t)
-        return carry
-
-    lax.fori_loop(0, 2, mirror_xy, 0)
+    lax.fori_loop(0, 4, diag, 0)
 
     for cx, cy in zip(out_x, out_y):
         tcopy(me, cx, at.x0, 0).wait_send()
@@ -396,17 +482,16 @@
 
     lax.fori_loop(0, nblk, sib_done, 0)
 
-    def costs(j, carry):
-        prod = jnp.dot(a_ref[...], tgt_ref[j], preferred_element_type=jnp.float32)
-        where = pl.ds(pl.multiple_of(j * BLK, BLK), BLK)
-        cost_ref[:, where] = cross_ref[:, where] - (2.0 * (1.0 - ALPHA)) * prod
-        return carry
-
-    def half(i):
-        part = pl.ds(i * (rows // 4), rows // 4)
-        return pltpu.make_async_remote_copy(
-            src_ref=kern_ref.at[0, part], dst_ref=kern_ref.at[1, part], send_sem=half_send.at[i],
-            recv_sem=half_recv.at[i], device_id={"rows": at.sib})
+    def a_done():
+        @pl.when(at.core == 0)
+        def _():
+            def body(j, carry):
+                a_copy(j).wait_send()
+                return carry
+
+            lax.fori_loop(0, nblk, body, 0)
+
+    a_done()
 
     def early(src, j, slot, dest, kind):
         return pltpu.make_async_remote_copy(
@@ -463,18 +548,11 @@
 
     def sweeps(first):
         reach = len(across) if first else 1
-        lax.fori_loop(0, nblk, costs, 0)
-        for i in range(4):
-            build_kernel(cost_ref, kern_ref, eps, i * (rows // 4), rows // 4, cols)
-
-            @pl.when(at.core == 0)
-            def _():
-                half(i).start()
+        build_kernel(cost_ref, kern_ref, eps, 0, rows, cols)
 
         @pl.when(at.core == 1)
         def _():
-            for i in range(4):
-                half(i).wait_recv()
+            build_kernel(cost_ref, kern_ref, eps, 1, rows, cols)
             sinkhorn(at, kern_ref, p_ref, q_ref, u_ref, v_ref, part_ref, gath_ref, sum_send, sum_recv)
             msg_ref[:tiles] = v_ref[...]
             msg_ref[tiles:] = jnp.zeros_like(msg_ref[tiles:])
@@ -490,8 +568,6 @@
         def _():
             if first:
                 early_round()
-            for i in range(4):
-                half(i).wait_send()
             for k in range(reach):
                 news(k).wait_recv()
             v_ref[...] = news_ref[0, :tiles]
@@ -512,20 +588,43 @@
     def form(k, j):
         return plan_block(lambda h: early_ref[k, j, :, h * LANES:(h + 1) * LANES], other_ref[k], v_ref, j)
 
-    gather_plan(at, nblk, plan_ref, plan_send, plan_recv, next_plan, lambda: None, column, form)
+    def add_column(j):
+        @pl.when(at.core == 1)
+        def _():
+            a_copy(j).wait_recv()
+
+        def go(reach):
+            def body(col, carry):
+                where = pl.ds(pl.multiple_of(col * BLK, BLK), BLK)
+
+                @pl.when(j == 0)
+                def _():
+                    cost_ref[:reach, where] = cross_ref[:reach, where] - term(reach, j, col)
+
+                @pl.when(j > 0)
+                def _():
+                    cost_ref[:reach, where] = cost_ref[:reach, where] - term(reach, j, col)
+
+                return carry
+
+            lax.fori_loop(0, nblk, body, 0)
+
+        on_reach(go)
+
+    def second_column(j):
+        make_column(j)
+
+        @pl.when(j > 0)
+        def _():
+            add_column(j - 1)
+
+    gather_plan(at, nblk, plan_ref, plan_send, plan_recv, next_plan, lambda: None, second_column, form)
+    add_column(nblk - 1)
+    a_done()
     sweeps(False)
 
-    def store(j):
-        return pltpu.make_async_copy(stage_ref.at[j], out_hbm.at[:, pl.ds(pl.multiple_of(j * BLK, BLK), BLK)], load_sem.at[j])
-
-    def last_plan(j, carry):
-        stage_ref[j] = own_block(j)
-        store(j).start()
-        return carry
-
-    lax.fori_loop(0, nblk, last_plan, 0)
     for j in range(nblk):
-        store(j).wait()
+        out_ref[:, j * BLK:(j + 1) * BLK] = own_block(j)
 
 
 def fgw(src, tgt, plan, mass, q, fsrc, ftgt, eps):
@@ -533,13 +632,13 @@
     tiles = cols // LANES
     nblk = cols // BLK
     vmem = pl.BlockSpec(memory_space=pltpu.VMEM)
-    hbm = pl.BlockSpec(memory_space=pl.ANY)
+    hbm = pl.BlockSpec(memory_space=pltpu.HBM)
     f32, bf16 = jnp.float32, jnp.bfloat16
     return pl.pallas_call(
         fgw_kernel,
         out_shape=jax.ShapeDtypeStruct((rows, cols), f32),
         in_specs=[pl.BlockSpec(memory_space=pltpu.SMEM), vmem, vmem] + [hbm] * 5,
-        out_specs=hbm,
+        out_specs=vmem,
         scratch_shapes=[
             pltpu.VMEM((nblk, BLK, BLK), f32),
             pltpu.VMEM((nblk, BLK, BLK), f32),
@@ -547,10 +646,10 @@
             pltpu.VMEM((nblk + 1, DEV * BLK, BLK), bf16),
             pltpu.VMEM((nblk, DEV * BLK, BLK), bf16),
             pltpu.VMEM((rows, cols), bf16),
-            pltpu.VMEM((BLK, BLK), bf16),
-            pltpu.VMEM((rows, cols), bf16),
-            pltpu.VMEM((rows, cols), f32),
-            pltpu.VMEM((rows, cols), f32),
+            pltpu.VMEM((2 * BLK, BLK), bf16),
+            pltpu.VMEM((2 * rows, cols), bf16),
+            pltpu.VMEM((2 * rows, cols), f32),
+            pltpu.VMEM((2 * rows, cols), f32),
             pltpu.VMEM((2, rows, cols), f32),
             pltpu.VMEM((3, EARLY, BLK, BLK), f32),
             pltpu.VMEM((2 * rows, LANES), f32),
@@ -569,14 +668,16 @@
             pltpu.SemaphoreType.DMA((DEV, nblk)),
             pltpu.SemaphoreType.DMA((2, 3)),
             pltpu.SemaphoreType.DMA((2, DEV // 2)),
-            pltpu.SemaphoreType.DMA((5,)),
-            pltpu.SemaphoreType.DMA((5,)),
+            pltpu.SemaphoreType.DMA((nblk,)),
+            pltpu.SemaphoreType.DMA((nblk,)),
+            pltpu.SemaphoreType.DMA((2,)),
+            pltpu.SemaphoreType.DMA((2,)),
             pltpu.SemaphoreType.DMA((3, EARLY)),
             pltpu.SemaphoreType.DMA((3, EARLY)),
             pltpu.SemaphoreType.DMA((4,)),
             pltpu.SemaphoreType.DMA((4,)),
         ],
-        compiler_params=pltpu.CompilerParams(collective_id=0, has_side_effects=True, vmem_limit_bytes=60 << 20),
+        compiler_params=pltpu.CompilerParams(collective_id=0, has_side_effects=True, vmem_limit_bytes=50 << 20),
         name="fgw",
     )(eps, mass, q, src, tgt, plan, fsrc, ftgt)
 

time: 172 us -> 175 us (1.017)
    unnamed x1 -> x9, local copies, waits for them, and re-layouts: 3.14 us -> 4.59 us
where the time goes in v4:
time: 175 us
  Pallas kernels  169 us (97%)
  local copies, waits for them, and re-layouts  4.59 us (3%)
    pallas_call x1, Pallas kernels, fgw(): pl.pallas_call(fgw_kernel, out_shape=jax.ShapeDtypeStruct((rows, cols), f...  169 us
    unnamed x9, local copies, waits for them, and re-layouts  4.59 us

profile of v4, /device:TPU:0, one launch (start us, length us, event | category | flops | bytes accessed | tf_op | source)
XLA Modules:
  0.0 174.6 jit_solution(8604544158338708249)
XLA Ops:
  0.7 0.0 copy-start
  0.7 0.9 copy-done
  1.6 0.0 copy-start.1
  1.6 0.9 copy-done.1
  2.6 0.0 copy-start.2
  2.6 0.7 copy-done.2
  3.3 0.0 copy-start.3
  3.3 0.7 copy-done.3
  3.9 169.3 %fgw.1 = f32[256,2048]{1,0:T(8,128)S(1)} custom-call(f32[1]{0:T(128)} %bitcast.3.eps_ref, f32[2,128]{1,0:T(2,128)S(1)} %bitcast.5, f32[16,128]{1,0:T(8,128)S(1)} %bitcast.4, f32[256,2048]{1,0:T(8,128)} %src_hbm.1, f32[256,2048]{1,0:T(8,128)} %tgt_hbm.1, f32[256,2048]{1,0:T(8,128)} %plan_hbm.1, f32[256,256]{1,0:T(8,128)S(1)} %copy-done, f32[256,256]{1,0:T(8,128)S(1)} %copy-done.1), custom_call_target="tpu_custom_call" | custom-call | tf_op jit(solution)/shard_map/fgw/pallas_call | solution.py:637
  173.2 1.3 copy.11
Async XLA Ops:
  0.7 1.0 copy-start
  1.6 0.9 copy-start.1
  2.6 0.7 copy-start.2
  3.3 0.7 copy-start.3

commit v5 on v4

--- a/solution.py
+++ b/solution.py
@@ -57,7 +57,7 @@
             kern_ref[half, pl.ds(row, SUB), t * LANES:(t + 1) * LANES] = jnp.exp((low - vals[t]) * inv_eps)
         return carry
 
-    lax.fori_loop(0, rows // SUB, block, 0, unroll=4)
+    lax.fori_loop(0, rows // SUB, block, 0, unroll=8)
 
 
 def spread(line, eye):
@@ -120,7 +120,7 @@
     return jnp.concatenate(parts, axis=1)
 
 
-def gather_plan(at, chunks, plan_ref, send_sem, recv_sem, produce, near_end, column, form=None):
+def gather_plan(at, chunks, plan_ref, send_sem, recv_sem, produce, column, form=None):
     def copy(owner, j, dest, kind):
         view = plan_ref.at[j, rows_of(owner), :]
         return pltpu.make_async_remote_copy(
@@ -141,9 +141,10 @@
 
         copy(at.me, j, at.sib, 2).start()
 
-    for j in range(AHEAD):
-        produce(j)
-        send_own(j)
+    def begin():
+        for j in range(AHEAD):
+            produce(j)
+            send_own(j)
 
     def turn(it, carry):
         @pl.when(it + AHEAD < chunks)
@@ -173,10 +174,6 @@
                 for k, owner in enumerate((at.x0, at.y0, at.d0)):
                     plan_ref[it, rows_of(owner), :] = form(k, it).astype(jnp.bfloat16)
                     copy(owner, it, at.sib, 3 + k).start()
-
-        @pl.when(it == chunks - 1)
-        def _():
-            near_end()
 
         @pl.when((it >= LAG) & (it < LAG + chunks) & over_links(it - LAG))
         def _():
@@ -192,8 +189,6 @@
 
         return carry
 
-    lax.fori_loop(0, chunks + LAG + 1, turn, 0)
-
     def drain(j, carry):
         for kind in (2, 3, 4, 5):
             copy(at.me, j, at.sib, kind).wait_send()
@@ -205,15 +200,19 @@
 
         return carry
 
-    lax.fori_loop(0, chunks, drain, 0)
+    def go_on():
+        lax.fori_loop(0, chunks + LAG + 1, turn, 0)
+        lax.fori_loop(0, chunks, drain, 0)
+
+    return begin, go_on
 
 
 def fgw_kernel(
-    eps_ref, mass_ref, q_ref, src_hbm, tgt_hbm, plan_hbm, fsrc_hbm, ftgt_hbm, out_ref,
-    stage_ref, stage2_ref, feat_ref, plan_ref, tgt_ref, src_ref, fsrc_ref, a_ref, cross_ref, cost_ref, kern_ref,
-    early_ref, p_ref, u_ref, v_ref, other_ref, part_ref, gath_ref, msg_ref, news_ref, mass2_ref,
-    load_sem, plan_send, plan_recv, tgt_send, tgt_recv, sum_send, sum_recv, a_send, a_recv, swap_send, swap_recv,
-    early_send, early_recv, msg_send, msg_recv,
+    eps_ref, mass_hbm, q_hbm, src_hbm, tgt_hbm, plan_hbm, fsrc_hbm, ftgt_hbm, out_ref,
+    stage_ref, stage2_ref, feat_ref, plan_ref, tgt_ref, src_ref, fsrc_ref, ftgt_ref, a_ref, cross_ref, cost_ref, kern_ref,
+    early_ref, p_ref, q_ref, u_ref, v_ref, other_ref, part_ref, gath_ref, msg_ref, news_ref, mass_ref, mass2_ref,
+    load_sem, plan_send, plan_recv, tgt_send, tgt_recv, feat_send, feat_recv, sum_send, sum_recv, a_send, a_recv,
+    swap_send, swap_recv, early_send, early_recv, msg_send, msg_recv,
 ):
     at = Place()
     me = at.me
@@ -230,57 +229,31 @@
     load_feat = pltpu.make_async_copy(ftgt_hbm, feat_ref.at[0], load_sem.at[2 * nblk])
     load_fsrc = pltpu.make_async_copy(fsrc_hbm, feat_ref.at[1], load_sem.at[2 * nblk + 1])
     load_src = pltpu.make_async_copy(src_hbm, cost_ref.at[:rows], load_sem.at[2 * nblk + 2])
-
-    for j in range(nblk):
-        load_plan(j).start()
-    load_feat.start()
-    load_fsrc.start()
-    load_src.start()
-    for j in range(nblk):
-        load_tgt(j).start()
+    load_mass = pltpu.make_async_copy(mass_hbm, mass_ref, load_sem.at[2 * nblk + 3])
+    load_q = pltpu.make_async_copy(q_hbm, q_ref, load_sem.at[2 * nblk + 4])
 
     barrier = pltpu.get_barrier_semaphore()
     for off in range(1, DEV):
         pl.semaphore_signal(barrier, inc=1, device_id={"rows": lax.rem(me + off, DEV)})
 
+    order = (me, at.sib, at.y0, at.x0, at.y1, at.x1, at.d0, at.d1)
+    for j in order:
+        load_tgt(j).start()
+    load_feat.start()
+    load_mass.start()
+    load_q.start()
+    load_fsrc.start()
+    for j in range(nblk):
+        load_plan(j).start()
+    load_src.start()
+
+    def cast_tgt(j):
+        load_tgt(j).wait()
+        tgt_ref[j, rows_of(me), :] = stage2_ref[j].astype(jnp.bfloat16)
+
+    cast_tgt(me)
+    cast_tgt(at.sib)
     pl.semaphore_wait(barrier, DEV - 1)
-
-    swap = pltpu.make_async_remote_copy(
-        src_ref=mass_ref, dst_ref=mass2_ref, send_sem=swap_send.at[0], recv_sem=swap_recv.at[0], device_id={"rows": at.sib})
-    swap.start()
-    swap_feat = pltpu.make_async_remote_copy(
-        src_ref=fsrc_ref.at[:BLK], dst_ref=fsrc_ref.at[BLK:], send_sem=swap_send.at[1], recv_sem=swap_recv.at[1],
-        device_id={"rows": at.sib})
-    eye = lax.broadcasted_iota(jnp.int32, (LANES, LANES), 0) == lax.broadcasted_iota(jnp.int32, (LANES, LANES), 1)
-
-    def cast_plan(j):
-        if isinstance(j, int):
-            load_plan(j).wait()
-            plan_ref[j, rows_of(me), :] = stage_ref[j].astype(jnp.bfloat16)
-            return
-
-        @pl.when(j < nblk)
-        def _():
-            load_plan(j).wait()
-            plan_ref[j, rows_of(me), :] = stage_ref[j].astype(jnp.bfloat16)
-
-        @pl.when(j == nblk)
-        def _():
-            load_feat.wait()
-            plan_ref[nblk, rows_of(me), :] = feat_ref[0].astype(jnp.bfloat16)
-
-        @pl.when(j == AHEAD)
-        def _():
-            load_fsrc.wait()
-            fsrc_ref[:BLK] = feat_ref[1].astype(jnp.bfloat16)
-            swap_feat.start()
-            load_src.wait()
-            src_ref[...] = cost_ref[:rows, :].astype(jnp.bfloat16)
-
-        @pl.when(j < nblk)
-        def _():
-            load_tgt(j).wait()
-            tgt_ref[j, rows_of(me), :] = stage2_ref[j].astype(jnp.bfloat16)
 
     def tcopy(owner, col, dest, kind):
         view = tgt_ref.at[col, rows_of(owner), :]
@@ -288,24 +261,59 @@
             src_ref=view, dst_ref=view, send_sem=tgt_send.at[kind, col],
             recv_sem=tgt_recv.at[owner, col], device_id={"rows": dest})
 
+    def fcopy(owner, dest, kind):
+        view = ftgt_ref.at[rows_of(owner), :]
+        return pltpu.make_async_remote_copy(
+            src_ref=view, dst_ref=view, send_sem=feat_send.at[kind], recv_sem=feat_recv.at[owner], device_id={"rows": dest})
+
     out_x = (at.me, at.sib, at.y0, at.y1, at.d0)
     out_y = (at.me, at.sib, at.x0, at.x1, at.d1)
     in_x = (at.x0, at.x1, at.d0, at.d1, at.y0)
     in_y = (at.y0, at.y1, at.d0, at.d1, at.x1)
 
-    def send_tgt():
-        for j in range(AHEAD):
-            load_tgt(j).wait()
-            tgt_ref[j, rows_of(me), :] = stage2_ref[j].astype(jnp.bfloat16)
-        for cx, cy in zip(out_x, out_y):
-            tcopy(me, cx, at.x0, 0).start()
-            tcopy(me, cy, at.y0, 1).start()
-
-        def to_sib(j, carry):
-            tcopy(me, j, at.sib, 2).start()
-            return carry
-
-        lax.fori_loop(0, nblk, to_sib, 0)
+    for k in range(2):
+        tcopy(me, out_x[k], at.x0, 0).start()
+        tcopy(me, out_y[k], at.y0, 1).start()
+        tcopy(me, out_x[k], at.sib, 2).start()
+    load_feat.wait()
+    ftgt_ref[rows_of(me), :] = feat_ref[0].astype(jnp.bfloat16)
+    fcopy(me, at.x0, 0).start()
+    fcopy(me, at.y0, 1).start()
+    fcopy(me, at.sib, 2).start()
+    for j in order[2:]:
+        cast_tgt(j)
+        tcopy(me, j, at.sib, 2).start()
+    for k in range(2, 5):
+        tcopy(me, out_x[k], at.x0, 0).start()
+        tcopy(me, out_y[k], at.y0, 1).start()
+
+    load_mass.wait()
+    load_q.wait()
+    swap = pltpu.make_async_remote_copy(
+        src_ref=mass_ref, dst_ref=mass2_ref, send_sem=swap_send.at[0], recv_sem=swap_recv.at[0], device_id={"rows": at.sib})
+    swap.start()
+    load_fsrc.wait()
+    fsrc_ref[:BLK] = feat_ref[1].astype(jnp.bfloat16)
+    swap_feat = pltpu.make_async_remote_copy(
+        src_ref=fsrc_ref.at[:BLK], dst_ref=fsrc_ref.at[BLK:], send_sem=swap_send.at[1], recv_sem=swap_recv.at[1],
+        device_id={"rows": at.sib})
+    swap_feat.start()
+    load_src.wait()
+    src_ref[...] = cost_ref[:rows, :].astype(jnp.bfloat16)
+    eye = lax.broadcasted_iota(jnp.int32, (LANES, LANES), 0) == lax.broadcasted_iota(jnp.int32, (LANES, LANES), 1)
+    swap.wait()
+    for r in range(rows // LANES):
+        p_ref[r * LANES:(r + 1) * LANES, :] = spread(mass_ref[r:r + 1, :], eye)
+        p_ref[rows + r * LANES:rows + (r + 1) * LANES, :] = spread(mass2_ref[r:r + 1, :], eye)
+
+    def on_reach(f):
+        @pl.when(at.core == 1)
+        def _():
+            f(2 * rows)
+
+        @pl.when(at.core == 0)
+        def _():
+            f(rows)
 
     def a_copy(j):
         cols_at = pl.ds(pl.multiple_of(j * BLK, BLK), BLK)
@@ -313,7 +321,30 @@
             src_ref=a_ref.at[:rows, cols_at], dst_ref=a_ref.at[rows:, cols_at], send_sem=a_send.at[j],
             recv_sem=a_recv.at[j], device_id={"rows": at.sib})
 
-    def make_column(j):
+    def add_column(j):
+        @pl.when(at.core == 1)
+        def _():
+            a_copy(j).wait_recv()
+
+        def add(reach, base_ref):
+            lhs = a_ref[:reach, pl.ds(pl.multiple_of(j * BLK, BLK), BLK)]
+            for col in range(nblk):
+                where = slice(col * BLK, (col + 1) * BLK)
+                prod = jnp.dot(lhs, tgt_ref[col, rows_of(j), :], preferred_element_type=jnp.float32)
+                cost_ref[:reach, where] = base_ref[:reach, where] - (2.0 * (1.0 - ALPHA)) * prod
+
+        def go(reach):
+            @pl.when(j == 0)
+            def _():
+                add(reach, cross_ref)
+
+            @pl.when(j > 0)
+            def _():
+                add(reach, cost_ref)
+
+        on_reach(go)
+
+    def column(j):
         prod = jnp.dot(src_ref[...], plan_ref[j], preferred_element_type=jnp.float32)
         a_ref[:rows, pl.ds(pl.multiple_of(j * BLK, BLK), BLK)] = prod.astype(jnp.bfloat16)
 
@@ -321,83 +352,27 @@
         def _():
             a_copy(j).start()
 
-    def first_column(j):
-        @pl.when(j < nblk)
-        def _():
-            make_column(j)
-
-    gather_plan(at, nblk + 1, plan_ref, plan_send, plan_recv, cast_plan, send_tgt, first_column)
-
-    def on_reach(f):
-        @pl.when(at.core == 1)
-        def _():
-            f(2 * rows)
-
-        @pl.when(at.core == 0)
-        def _():
-            f(rows)
-
-    swap.wait()
-    swap_feat.wait()
-    for r in range(rows // LANES):
-        p_ref[r * LANES:(r + 1) * LANES, :] = spread(mass_ref[r:r + 1, :], eye)
-        p_ref[rows + r * LANES:rows + (r + 1) * LANES, :] = spread(mass2_ref[r:r + 1, :], eye)
-
-    def crosses(reach):
-        def cross(j, carry):
-            prod = lax.dot_general(
-                fsrc_ref[:reach, :], plan_ref[nblk, rows_of(j), :], (((1,), (1,)), ((), ())),
-                preferred_element_type=jnp.float32)
-            where = pl.ds(pl.multiple_of(j * BLK, BLK), BLK)
-            cross_ref[:reach, where] = (-2.0 * ALPHA) * prod
-            cost_ref[:reach, where] = (-2.0 * ALPHA) * prod
-            return carry
-
-        lax.fori_loop(0, nblk, cross, 0)
-
-    on_reach(crosses)
-
-    @pl.when(at.core == 1)
-    def _():
-        def arrived(j, carry):
-            a_copy(j).wait_recv()
-            return carry
-
-        lax.fori_loop(0, nblk, arrived, 0)
-
-    def term(reach, i, col):
-        lhs = a_ref[:reach, pl.ds(pl.multiple_of(i * BLK, BLK), BLK)]
-        prod = jnp.dot(lhs, tgt_ref[col, rows_of(i), :], preferred_element_type=jnp.float32)
-        return (2.0 * (1.0 - ALPHA)) * prod
-
-    def add(i, col):
-        def go(reach):
-            where = pl.ds(pl.multiple_of(col * BLK, BLK), BLK)
-            cost_ref[:reach, where] = cost_ref[:reach, where] - term(reach, i, col)
-
-        on_reach(go)
+        @pl.when(j > 0)
+        def _():
+            add_column(j - 1)
+
+    def cast_plan(j):
+        load_plan(j).wait()
+        plan_ref[j, rows_of(me), :] = stage_ref[j].astype(jnp.bfloat16)
+
+    begin, go_on = gather_plan(at, nblk, plan_ref, plan_send, plan_recv, cast_plan, column)
 
     def mirror(owner, col):
         tgt_ref[owner, rows_of(col), :] = tgt_ref[col, rows_of(owner), :].T
 
-    def use(owner, col, paired):
-        add(owner, col)
-
-        @pl.when(paired)
-        def _():
-            mirror(owner, col)
-            add(col, owner)
-
     base = me - at.core
 
-    def use_row(owner):
+    def mirror_row(owner):
         def body(t, carry):
-            use(owner, lax.rem(base + t, DEV), t >= 2)
+            mirror(owner, lax.rem(base + 2 + t, DEV))
             return carry
 
-        lax.fori_loop(0, DEV, body, 0)
-
-    use_row(me)
+        lax.fori_loop(0, DEV - 2, body, 0)
 
     def stream(k, s, other):
         core = lax.rem(at.core + other, 2)
@@ -423,25 +398,50 @@
                 def _():
                     tcopy(at.y0, at.y0, at.x0, 6).start()
 
-        @pl.when(k == 0)
-        def _():
+        @pl.when(k == 1)
+        def _():
+            fcopy(at.x0, at.sib, 0).wait_recv()
+            fcopy(at.x0, at.sib, 3).start()
+            fcopy(at.y0, at.sib, 0).wait_recv()
+            fcopy(at.y0, at.sib, 4).start()
+
+            @pl.when(at.core == 0)
+            def _():
+                fcopy(at.x0, at.y0, 6).start()
+
+            @pl.when(at.core == 1)
+            def _():
+                fcopy(at.y0, at.x0, 6).start()
+
+            mirror_row(me)
+
+        @pl.when(k == 2)
+        def _():
+            begin()
+
             def from_sib(j, c):
                 tcopy(at.sib, j, at.sib, 0).wait_recv()
                 return c
 
             lax.fori_loop(0, nblk, from_sib, 0)
-            use_row(at.sib)
-
-        def near(s, c):
-            use(*stream(k, s, 0), k >= 2)
-            return c
-
-        lax.fori_loop(0, 2, near, 0)
+            mirror_row(at.sib)
+
+        @pl.when(k >= 2)
+        def _():
+            def near(s, c):
+                mirror(*stream(k, s, 0))
+                return c
+
+            lax.fori_loop(0, 2, near, 0)
 
         def near_other(s, c):
             owner, col = stream(k, s, 1)
             tcopy(owner, col, at.sib, 0).wait_recv()
-            use(owner, col, k >= 2)
+
+            @pl.when(k >= 2)
+            def _():
+                mirror(owner, col)
+
             return c
 
         lax.fori_loop(0, 2, near_other, 0)
@@ -451,20 +451,31 @@
     for col in (at.d0, at.d1):
         tcopy(at.d0, col, at.d0, 0).wait_recv()
         tcopy(at.d0, col, at.sib, 5).start()
-
-    def diag(t, carry):
-        owner = at.d0 + (t // 2) * (at.d1 - at.d0)
-        col = at.d0 + lax.rem(t, 2) * (at.d1 - at.d0)
-
-        @pl.when(t >= 2)
-        def _():
-            tcopy(owner, col, at.sib, 0).wait_recv()
-
-        add(owner, col)
-        return carry
-
-    lax.fori_loop(0, 4, diag, 0)
-
+    fcopy(at.d0, at.sib, 0).wait_recv()
+    fcopy(at.d0, at.sib, 5).start()
+    for owner in (at.sib, at.x1, at.y1, at.d1):
+        fcopy(owner, at.sib, 0).wait_recv()
+    swap_feat.wait()
+
+    def crosses(reach):
+        def cross(j, carry):
+            prod = lax.dot_general(
+                fsrc_ref[:reach, :], ftgt_ref[rows_of(j), :], (((1,), (1,)), ((), ())),
+                preferred_element_type=jnp.float32)
+            cross_ref[:reach, pl.ds(pl.multiple_of(j * BLK, BLK), BLK)] = (-2.0 * ALPHA) * prod
+            return carry
+
+        lax.fori_loop(0, nblk, cross, 0)
+
+    on_reach(crosses)
+    for col in (at.d1, at.d0):
+        tcopy(at.d1, col, at.sib, 0).wait_recv()
+
+    go_on()
+    add_column(nblk - 1)
+
+    for kind in range(7):
+        fcopy(me, at.sib, kind).wait_send()
     for cx, cy in zip(out_x, out_y):
         tcopy(me, cx, at.x0, 0).wait_send()
         tcopy(me, cy, at.y0, 1).wait_send()
@@ -588,37 +599,9 @@
     def form(k, j):
         return plan_block(lambda h: early_ref[k, j, :, h * LANES:(h + 1) * LANES], other_ref[k], v_ref, j)
 
-    def add_column(j):
-        @pl.when(at.core == 1)
-        def _():
-            a_copy(j).wait_recv()
-
-        def go(reach):
-            def body(col, carry):
-                where = pl.ds(pl.multiple_of(col * BLK, BLK), BLK)
-
-                @pl.when(j == 0)
-                def _():
-                    cost_ref[:reach, where] = cross_ref[:reach, where] - term(reach, j, col)
-
-                @pl.when(j > 0)
-                def _():
-                    cost_ref[:reach, where] = cost_ref[:reach, where] - term(reach, j, col)
-
-                return carry
-
-            lax.fori_loop(0, nblk, body, 0)
-
-        on_reach(go)
-
-    def second_column(j):
-        make_column(j)
-
-        @pl.when(j > 0)
-        def _():
-            add_column(j - 1)
-
-    gather_plan(at, nblk, plan_ref, plan_send, plan_recv, next_plan, lambda: None, second_column, form)
+    begin, go_on = gather_plan(at, nblk, plan_ref, plan_send, plan_recv, next_plan, column, form)
+    begin()
+    go_on()
     add_column(nblk - 1)
     a_done()
     sweeps(False)
@@ -637,22 +620,24 @@
     return pl.pallas_call(
         fgw_kernel,
         out_shape=jax.ShapeDtypeStruct((rows, cols), f32),
-        in_specs=[pl.BlockSpec(memory_space=pltpu.SMEM), vmem, vmem] + [hbm] * 5,
+        in_specs=[pl.BlockSpec(memory_space=pltpu.SMEM)] + [hbm] * 7,
         out_specs=vmem,
         scratch_shapes=[
             pltpu.VMEM((nblk, BLK, BLK), f32),
             pltpu.VMEM((nblk, BLK, BLK), f32),
             pltpu.VMEM((2, BLK, BLK), f32),
-            pltpu.VMEM((nblk + 1, DEV * BLK, BLK), bf16),
+            pltpu.VMEM((nblk, DEV * BLK, BLK), bf16),
             pltpu.VMEM((nblk, DEV * BLK, BLK), bf16),
             pltpu.VMEM((rows, cols), bf16),
             pltpu.VMEM((2 * BLK, BLK), bf16),
+            pltpu.VMEM((DEV * BLK, BLK), bf16),
             pltpu.VMEM((2 * rows, cols), bf16),
             pltpu.VMEM((2 * rows, cols), f32),
             pltpu.VMEM((2 * rows, cols), f32),
             pltpu.VMEM((2, rows, cols), f32),
             pltpu.VMEM((3, EARLY, BLK, BLK), f32),
             pltpu.VMEM((2 * rows, LANES), f32),
+            pltpu.VMEM((tiles, LANES), f32),
             pltpu.VMEM((2 * rows, LANES), f32),
             pltpu.VMEM((tiles, LANES), f32),
             pltpu.VMEM((3, rows, LANES), f32),
@@ -661,11 +646,14 @@
             pltpu.VMEM((tiles + SUB, LANES), f32),
             pltpu.VMEM((4, tiles + SUB, LANES), f32),
             pltpu.VMEM((rows // LANES, LANES), f32),
-            pltpu.SemaphoreType.DMA((2 * nblk + 3,)),
-            pltpu.SemaphoreType.DMA((7, nblk + 1)),
-            pltpu.SemaphoreType.DMA((DEV, nblk + 1)),
+            pltpu.VMEM((rows // LANES, LANES), f32),
+            pltpu.SemaphoreType.DMA((2 * nblk + 5,)),
             pltpu.SemaphoreType.DMA((7, nblk)),
             pltpu.SemaphoreType.DMA((DEV, nblk)),
+            pltpu.SemaphoreType.DMA((7, nblk)),
+            pltpu.SemaphoreType.DMA((DEV, nblk)),
+            pltpu.SemaphoreType.DMA((7,)),
+            pltpu.SemaphoreType.DMA((DEV,)),
             pltpu.SemaphoreType.DMA((2, 3)),
             pltpu.SemaphoreType.DMA((2, DEV // 2)),
             pltpu.SemaphoreType.DMA((nblk,)),
@@ -679,7 +667,7 @@
         ],
         compiler_params=pltpu.CompilerParams(collective_id=0, has_side_effects=True, vmem_limit_bytes=50 << 20),
         name="fgw",
-    )(eps, mass, q, src, tgt, plan, fsrc, ftgt)
+    )(eps, *[pltpu.with_memory_space_constraint(x, pltpu.HBM) for x in (mass, q, src, tgt, plan, fsrc, ftgt)])
 
 
 def solution(mesh):

time: 175 us -> 161 us (0.920)
  Pallas kernels: 169 us -> 159 us
  local copies, waits for them, and re-layouts: 4.59 us -> 1.32 us
    pallas_call x1, Pallas kernels: 169 us -> 159 us  [fgw(): pl.pallas_call(fgw_kernel, out_shape=jax.ShapeDtypeStruct((rows, cols), f...]
    unnamed x9 -> x1, local copies, waits for them, and re-layouts: 4.59 us -> 1.32 us
where the time goes in v5:
time: 161 us
  Pallas kernels  159 us (99%)
    pallas_call x1, Pallas kernels, fgw(): pl.pallas_call(fgw_kernel, out_shape=jax.ShapeDtypeStruct((rows, cols), f...  159 us

profile of v5, /device:TPU:0, one launch (start us, length us, event | category | flops | bytes accessed | tf_op | source)
XLA Modules:
  0.0 160.7 jit_solution(2915449603875120835)
XLA Ops:
  0.7 158.7 %fgw.1 = f32[256,2048]{1,0:T(8,128)S(1)} custom-call(f32[1]{0:T(128)} %bitcast.3.eps_ref, f32[2,128]{1,0:T(2,128)} %bitcast.5, f32[16,128]{1,0:T(8,128)} %bitcast.4, f32[256,2048]{1,0:T(8,128)} %src_hbm.1, f32[256,2048]{1,0:T(8,128)} %tgt_hbm.1, f32[256,2048]{1,0:T(8,128)} %plan_hbm.1, f32[256,256]{1,0:T(8,128)} %fsrc_hbm.1, f32[256,256]{1,0:T(8,128)} %ftgt_hbm.1), custom_call_target="tpu_custom_call" | custom-call | tf_op jit(solution)/shard_map/fgw/pallas_call | solution.py:620
  159.4 1.3 copy.11

commit v6 on v5

--- a/solution.py
+++ b/solution.py
@@ -17,6 +17,7 @@
 AHEAD = 2
 LAG = 2
 EARLY = 7
+PIECES = 2
 
 
 def tree_sum(vals):
@@ -66,50 +67,85 @@
     return jnp.broadcast_to(col, (LANES, LANES))
 
 
-def sinkhorn(at, kern_ref, p_ref, q_ref, u_ref, v_ref, part_ref, gath_ref, send_sem, recv_sem):
+def sinkhorn(at, kern_ref, p_ref, q_ref, u_ref, v_ref, dots_ref, part_ref, gath_ref, send_sem, recv_sem):
     halves, rows, cols = kern_ref.shape
     tiles = cols // LANES
+    span = tiles // PIECES
     blocks = [(h, b) for h in range(halves) for b in range(rows // SUB)]
     chip = at.me // 2
     peers = (at.x0, at.y0, at.d0)
 
-    def copy(par, k, slot):
+    def copy(par, g, k, slot):
         return pltpu.make_async_remote_copy(
-            src_ref=part_ref.at[par], dst_ref=gath_ref.at[par, slot],
-            send_sem=send_sem.at[par, k], recv_sem=recv_sem.at[par, slot], device_id={"rows": peers[k]})
+            src_ref=part_ref.at[par, g], dst_ref=gath_ref.at[par, g, slot],
+            send_sem=send_sem.at[par, g, k], recv_sem=recv_sem.at[par, g, slot], device_id={"rows": peers[k]})
+
+    def tile(h, b, t):
+        return kern_ref[h, b * SUB:(b + 1) * SUB, t * LANES:(t + 1) * LANES]
+
+    def at_row(h, b):
+        return slice(h * rows + b * SUB, h * rows + (b + 1) * SUB)
+
+    def dots_of(g):
+        vrow = [jnp.broadcast_to(v_ref[t:t + 1, :], (SUB, LANES)) for t in range(g * span, (g + 1) * span)]
+        for h, b in blocks:
+            dots = tree_sum([tile(h, b, g * span + t) * vrow[t] for t in range(span)])
+            if g > 0:
+                dots = dots + dots_ref[at_row(h, b), :]
+            if g < PIECES - 1:
+                dots_ref[at_row(h, b), :] = dots
+            else:
+                u_ref[at_row(h, b), :] = p_ref[at_row(h, b), :] / jnp.sum(dots, axis=1, keepdims=True)
+
+    def sums_of(par, g):
+        acc = [None] * span
+        for h, b in blocks:
+            scale = u_ref[at_row(h, b), :]
+            for t in range(span):
+                term = tile(h, b, g * span + t) * scale
+                acc[t] = term if acc[t] is None else acc[t] + term
+        sums = jnp.concatenate([jnp.sum(a, axis=0, keepdims=True) for a in acc], axis=0)
+        part_ref[par, g] = sums
+        for k in (2, 0, 1):
+            copy(par, g, k, chip).start()
+        gath_ref[par, g, chip] = sums
+
+    def scales_of(par, g):
+        for k in range(3):
+            copy(par, g, k, peers[k] // 2).wait_recv()
+        total = gath_ref[par, g, 0]
+        for d in range(1, DEV // 2):
+            total = total + gath_ref[par, g, d]
+        v_ref[g * span:(g + 1) * span, :] = q_ref[g * span:(g + 1) * span, :] / total
+
+    def sent(par):
+        for g in range(PIECES):
+            for k in range(3):
+                copy(par, g, k, chip).wait_send()
 
     v_ref[...] = jnp.ones_like(v_ref)
 
     def sweep(step, carry):
         par = lax.rem(step, 2)
-        vrow = [jnp.broadcast_to(v_ref[t:t + 1, :], (SUB, LANES)) for t in range(tiles)]
-        for h, b in blocks:
-            prods = [kern_ref[h, b * SUB:(b + 1) * SUB, t * LANES:(t + 1) * LANES] * vrow[t] for t in range(tiles)]
-            dots = jnp.sum(tree_sum(prods), axis=1, keepdims=True)
-            at_row = slice(h * rows + b * SUB, h * rows + (b + 1) * SUB)
-            u_ref[at_row, :] = p_ref[at_row, :] / dots
-        acc = [None] * tiles
-        for h, b in blocks:
-            scale = u_ref[h * rows + b * SUB:h * rows + (b + 1) * SUB, :]
-            for t in range(tiles):
-                term = kern_ref[h, b * SUB:(b + 1) * SUB, t * LANES:(t + 1) * LANES] * scale
-                acc[t] = term if acc[t] is None else acc[t] + term
-        sums = jnp.concatenate([jnp.sum(a, axis=0, keepdims=True) for a in acc], axis=0)
-        part_ref[par] = sums
-        for k in (2, 0, 1):
-            copy(par, k, chip).start()
-        gath_ref[par, chip] = sums
-        for k in range(3):
-            copy(par, k, peers[k] // 2).wait_recv()
-        total = gath_ref[par, 0]
-        for d in range(1, DEV // 2):
-            total = total + gath_ref[par, d]
-        v_ref[...] = q_ref[...] / total
-        for k in range(3):
-            copy(par, k, chip).wait_send()
+        for g in range(PIECES):
+            @pl.when(step > 0)
+            def _():
+                scales_of(1 - par, g)
+
+            dots_of(g)
+
+        @pl.when(step > 0)
+        def _():
+            sent(1 - par)
+
+        for g in range(PIECES):
+            sums_of(par, g)
         return carry
 
     lax.fori_loop(0, SWEEPS, sweep, 0)
+    for g in range(PIECES):
+        scales_of((SWEEPS - 1) % 2, g)
+    sent((SWEEPS - 1) % 2)
 
 
 def plan_block(kern, scale, v_ref, j):
@@ -210,7 +246,7 @@
 def fgw_kernel(
     eps_ref, mass_hbm, q_hbm, src_hbm, tgt_hbm, plan_hbm, fsrc_hbm, ftgt_hbm, out_ref,
     stage_ref, stage2_ref, feat_ref, plan_ref, tgt_ref, src_ref, fsrc_ref, ftgt_ref, a_ref, cross_ref, cost_ref, kern_ref,
-    early_ref, p_ref, q_ref, u_ref, v_ref, other_ref, part_ref, gath_ref, msg_ref, news_ref, mass_ref, mass2_ref,
+    early_ref, p_ref, q_ref, u_ref, v_ref, dots_ref, other_ref, part_ref, gath_ref, msg_ref, news_ref, mass_ref, mass2_ref,
     load_sem, plan_send, plan_recv, tgt_send, tgt_recv, feat_send, feat_recv, sum_send, sum_recv, a_send, a_recv,
     swap_send, swap_recv, early_send, early_recv, msg_send, msg_recv,
 ):
@@ -509,6 +545,12 @@
             src_ref=src, dst_ref=early_ref.at[slot, j], send_sem=early_send.at[kind, j],
             recv_sem=early_recv.at[slot, j], device_id={"rows": dest})
 
+    def early_half(i, dest):
+        part = pl.ds(i * (BLK // 2), BLK // 2)
+        return pltpu.make_async_remote_copy(
+            src_ref=early_ref.at[i, EARLY - 1, part], dst_ref=early_ref.at[2, EARLY - 1, part],
+            send_sem=early_send.at[2, EARLY - 1 + i], recv_sem=early_recv.at[2, EARLY - 1 + i], device_id={"rows": dest})
+
     def own_part(j):
         return kern_ref.at[0, :, pl.ds(pl.multiple_of(j * BLK, BLK), BLK)]
 
@@ -527,27 +569,43 @@
 
             early(own_part(j), j, 0, at.x0, 0).wait_recv()
 
-            @pl.when(lax.rem(j, 2) == 0)
+            @pl.when((lax.rem(j, 2) == 0) & (j < EARLY - 1))
             def _():
                 early(early_ref.at[0, j], j, 2, at.y0, 2).start()
 
+            @pl.when(j == EARLY - 1)
+            def _():
+                early_half(0, at.y0).start()
+
             early(own_part(j), j, 1, at.y0, 1).wait_recv()
 
-            @pl.when(lax.rem(j, 2) == 1)
+            @pl.when((lax.rem(j, 2) == 1) & (j < EARLY - 1))
             def _():
                 early(early_ref.at[1, j], j, 2, at.x0, 2).start()
 
+            @pl.when(j == EARLY - 1)
+            def _():
+                early_half(1, at.x0).start()
+
             return carry
 
         lax.fori_loop(0, EARLY, turn, 0)
 
         def done(j, carry):
-            early(own_part(j), j, 2, at.x0, 2).wait_recv()
-            for kind in range(3):
+            for kind in range(2):
                 early(own_part(j), j, kind, at.x0, kind).wait_send()
+
+            @pl.when(j < EARLY - 1)
+            def _():
+                early(own_part(j), j, 2, at.x0, 2).wait_recv()
+                early(own_part(j), j, 2, at.x0, 2).wait_send()
+
             return carry
 
         lax.fori_loop(0, EARLY, done, 0)
+        for i in range(2):
+            early_half(i, at.x0).wait_recv()
+            early_half(i, at.x0).wait_send()
 
     tiles = cols // LANES
     across = (at.sib, at.x1, at.y1, at.d1)
@@ -564,7 +622,7 @@
         @pl.when(at.core == 1)
         def _():
             build_kernel(cost_ref, kern_ref, eps, 1, rows, cols)
-            sinkhorn(at, kern_ref, p_ref, q_ref, u_ref, v_ref, part_ref, gath_ref, sum_send, sum_recv)
+            sinkhorn(at, kern_ref, p_ref, q_ref, u_ref, v_ref, dots_ref, part_ref, gath_ref, sum_send, sum_recv)
             msg_ref[:tiles] = v_ref[...]
             msg_ref[tiles:] = jnp.zeros_like(msg_ref[tiles:])
             for r in range(rows // LANES):
@@ -640,9 +698,10 @@
             pltpu.VMEM((tiles, LANES), f32),
             pltpu.VMEM((2 * rows, LANES), f32),
             pltpu.VMEM((tiles, LANES), f32),
+            pltpu.VMEM((2 * rows, LANES), f32),
             pltpu.VMEM((3, rows, LANES), f32),
-            pltpu.VMEM((2, tiles, LANES), f32),
-            pltpu.VMEM((2, DEV // 2, tiles, LANES), f32),
+            pltpu.VMEM((2, PIECES, tiles // PIECES, LANES), f32),
+            pltpu.VMEM((2, PIECES, DEV // 2, tiles // PIECES, LANES), f32),
             pltpu.VMEM((tiles + SUB, LANES), f32),
             pltpu.VMEM((4, tiles + SUB, LANES), f32),
             pltpu.VMEM((rows // LANES, LANES), f32),
@@ -654,14 +713,14 @@
             pltpu.SemaphoreType.DMA((DEV, nblk)),
             pltpu.SemaphoreType.DMA((7,)),
             pltpu.SemaphoreType.DMA((DEV,)),
-            pltpu.SemaphoreType.DMA((2, 3)),
-            pltpu.SemaphoreType.DMA((2, DEV // 2)),
+            pltpu.SemaphoreType.DMA((2, PIECES, 3)),
+            pltpu.SemaphoreType.DMA((2, PIECES, DEV // 2)),
             pltpu.SemaphoreType.DMA((nblk,)),
             pltpu.SemaphoreType.DMA((nblk,)),
             pltpu.SemaphoreType.DMA((2,)),
             pltpu.SemaphoreType.DMA((2,)),
-            pltpu.SemaphoreType.DMA((3, EARLY)),
-            pltpu.SemaphoreType.DMA((3, EARLY)),
+            pltpu.SemaphoreType.DMA((3, EARLY + 1)),
+            pltpu.SemaphoreType.DMA((3, EARLY + 1)),
             pltpu.SemaphoreType.DMA((4,)),
             pltpu.SemaphoreType.DMA((4,)),
         ],

time: 161 us -> 159 us (0.988)
  Pallas kernels: 159 us -> 157 us
    pallas_call x1, Pallas kernels: 159 us -> 157 us  [fgw(): pl.pallas_call(fgw_kernel, out_shape=jax.ShapeDtypeStruct((rows, cols), f...]
where the time goes in v6:
time: 159 us
  Pallas kernels  157 us (99%)
    pallas_call x1, Pallas kernels, fgw(): pl.pallas_call(fgw_kernel, out_shape=jax.ShapeDtypeStruct((rows, cols), f...  157 us

profile of v6, /device:TPU:0, one launch (start us, length us, event | category | flops | bytes accessed | tf_op | source)
XLA Modules:
  0.0 158.7 jit_solution(1686382920580948780)
XLA Ops:
  0.7 156.7 %fgw.1 = f32[256,2048]{1,0:T(8,128)S(1)} custom-call(f32[1]{0:T(128)} %bitcast.3.eps_ref, f32[2,128]{1,0:T(2,128)} %bitcast.5, f32[16,128]{1,0:T(8,128)} %bitcast.4, f32[256,2048]{1,0:T(8,128)} %src_hbm.1, f32[256,2048]{1,0:T(8,128)} %tgt_hbm.1, f32[256,2048]{1,0:T(8,128)} %plan_hbm.1, f32[256,256]{1,0:T(8,128)} %fsrc_hbm.1, f32[256,256]{1,0:T(8,128)} %ftgt_hbm.1), custom_call_target="tpu_custom_call" | custom-call | tf_op jit(solution)/shard_map/fgw/pallas_call | solution.py:678
  157.4 1.3 copy.11

commit v7 on v6

--- a/solution.py
+++ b/solution.py
@@ -307,10 +307,18 @@
     in_x = (at.x0, at.x1, at.d0, at.d1, at.y0)
     in_y = (at.y0, at.y1, at.d0, at.d1, at.x1)
 
-    for k in range(2):
-        tcopy(me, out_x[k], at.x0, 0).start()
-        tcopy(me, out_y[k], at.y0, 1).start()
-        tcopy(me, out_x[k], at.sib, 2).start()
+    def pair_send(wait):
+        for core, dest in ((0, at.x0), (1, at.y0)):
+            @pl.when(at.core == core)
+            def _():
+                copy = tcopy(me, at.sib, dest, core)
+                copy.wait_send() if wait else copy.start()
+
+    tcopy(me, me, at.x0, 0).start()
+    tcopy(me, me, at.y0, 1).start()
+    pair_send(False)
+    for col in (me, at.sib):
+        tcopy(me, col, at.sib, 2).start()
     load_feat.wait()
     ftgt_ref[rows_of(me), :] = feat_ref[0].astype(jnp.bfloat16)
     fcopy(me, at.x0, 0).start()
@@ -422,17 +430,19 @@
 
     def arrivals(k, carry):
         for s, fwd in ((0, 3), (1, 4)):
-            owner, col = stream(k, s, 0)
-            tcopy(owner, col, at.sib, 0).wait_recv()
-            tcopy(owner, col, at.sib, fwd).start()
-            if s == 0:
-                @pl.when(k == 1)
-                def _():
-                    tcopy(at.x0, at.x1, at.y0, 6).start()
-            else:
-                @pl.when(k == 0)
-                def _():
-                    tcopy(at.y0, at.y0, at.x0, 6).start()
+            @pl.when((k != 1) | (at.core == s))
+            def _():
+                owner, col = stream(k, s, 0)
+                tcopy(owner, col, at.sib, 0).wait_recv()
+                tcopy(owner, col, at.sib, fwd).start()
+
+        @pl.when(k == 0)
+        def _():
+            tcopy(at.y0, at.y0, at.x0, 6).start()
+
+        @pl.when((k == 1) & (at.core == 0))
+        def _():
+            tcopy(at.x0, at.x1, at.y0, 6).start()
 
         @pl.when(k == 1)
         def _():
@@ -462,31 +472,34 @@
             lax.fori_loop(0, nblk, from_sib, 0)
             mirror_row(at.sib)
 
-        @pl.when(k >= 2)
-        def _():
-            def near(s, c):
-                mirror(*stream(k, s, 0))
-                return c
-
-            lax.fori_loop(0, 2, near, 0)
-
-        def near_other(s, c):
-            owner, col = stream(k, s, 1)
-            tcopy(owner, col, at.sib, 0).wait_recv()
-
-            @pl.when(k >= 2)
-            def _():
-                mirror(owner, col)
+        def near(t, c):
+            other = t // 2
+            owner, col = stream(k, lax.rem(t, 2), other)
+
+            @pl.when((k != 1) | (lax.rem(at.core + other, 2) == lax.rem(t, 2)))
+            def _():
+                @pl.when(t >= 2)
+                def _():
+                    tcopy(owner, col, at.sib, 0).wait_recv()
+
+                @pl.when(k >= 1)
+                def _():
+                    mirror(owner, col)
 
             return c
 
-        lax.fori_loop(0, 2, near_other, 0)
+        lax.fori_loop(0, 4, near, 0)
         return carry
 
     lax.fori_loop(0, 5, arrivals, 0)
-    for col in (at.d0, at.d1):
-        tcopy(at.d0, col, at.d0, 0).wait_recv()
-        tcopy(at.d0, col, at.sib, 5).start()
+    tcopy(at.d0, at.d0, at.d0, 0).wait_recv()
+    tcopy(at.d0, at.d0, at.sib, 5).start()
+
+    @pl.when(at.core == 0)
+    def _():
+        tcopy(at.d0, at.d1, at.d0, 0).wait_recv()
+        tcopy(at.d0, at.d1, at.sib, 5).start()
+
     fcopy(at.d0, at.sib, 0).wait_recv()
     fcopy(at.d0, at.sib, 5).start()
     for owner in (at.sib, at.x1, at.y1, at.d1):
@@ -504,24 +517,37 @@
         lax.fori_loop(0, nblk, cross, 0)
 
     on_reach(crosses)
-    for col in (at.d1, at.d0):
-        tcopy(at.d1, col, at.sib, 0).wait_recv()
+    tcopy(at.d1, at.d1, at.sib, 0).wait_recv()
+
+    @pl.when(at.core == 1)
+    def _():
+        tcopy(at.d1, at.d0, at.sib, 0).wait_recv()
+
+    mirror(at.d0 - at.core, at.d0 - at.core + 1)
 
     go_on()
     add_column(nblk - 1)
 
     for kind in range(7):
         fcopy(me, at.sib, kind).wait_send()
-    for cx, cy in zip(out_x, out_y):
-        tcopy(me, cx, at.x0, 0).wait_send()
-        tcopy(me, cy, at.y0, 1).wait_send()
-    for k in range(5):
+    pair_send(True)
+    for k in (0, 2, 3, 4):
+        tcopy(me, out_x[k], at.x0, 0).wait_send()
+        tcopy(me, out_y[k], at.y0, 1).wait_send()
         tcopy(at.x0, in_x[k], at.sib, 3).wait_send()
         tcopy(at.y0, in_y[k], at.sib, 4).wait_send()
-    for col in (at.d0, at.d1):
-        tcopy(at.d0, col, at.sib, 5).wait_send()
-    tcopy(at.x0, at.x1, at.y0, 6).wait_send()
+    tcopy(at.d0, at.d0, at.sib, 5).wait_send()
     tcopy(at.y0, at.y0, at.x0, 6).wait_send()
+
+    @pl.when(at.core == 0)
+    def _():
+        tcopy(at.x0, at.x1, at.sib, 3).wait_send()
+        tcopy(at.d0, at.d1, at.sib, 5).wait_send()
+        tcopy(at.x0, at.x1, at.y0, 6).wait_send()
+
+    @pl.when(at.core == 1)
+    def _():
+        tcopy(at.y0, at.y1, at.sib, 4).wait_send()
 
     def sib_done(j, carry):
         tcopy(me, j, at.sib, 2).wait_send()

time: 159 us -> 156 us (0.981)
  Pallas kernels: 157 us -> 154 us
    pallas_call x1, Pallas kernels: 157 us -> 154 us  [fgw(): pl.pallas_call(fgw_kernel, out_shape=jax.ShapeDtypeStruct((rows, cols), f...]
where the time goes in v7:
time: 156 us
  Pallas kernels  154 us (99%)
    pallas_call x1, Pallas kernels, fgw(): pl.pallas_call(fgw_kernel, out_shape=jax.ShapeDtypeStruct((rows, cols), f...  154 us

profile of v7, /device:TPU:0, one launch (start us, length us, event | category | flops | bytes accessed | tf_op | source)
XLA Modules:
  0.0 156.2 jit_solution(5017428184884721436)
XLA Ops:
  0.7 154.3 %fgw.1 = f32[256,2048]{1,0:T(8,128)S(1)} custom-call(f32[1]{0:T(128)} %bitcast.3.eps_ref, f32[2,128]{1,0:T(2,128)} %bitcast.5, f32[16,128]{1,0:T(8,128)} %bitcast.4, f32[256,2048]{1,0:T(8,128)} %src_hbm.1, f32[256,2048]{1,0:T(8,128)} %tgt_hbm.1, f32[256,2048]{1,0:T(8,128)} %plan_hbm.1, f32[256,256]{1,0:T(8,128)} %fsrc_hbm.1, f32[256,256]{1,0:T(8,128)} %ftgt_hbm.1), custom_call_target="tpu_custom_call" | custom-call | tf_op jit(solution)/shard_map/fgw/pallas_call | solution.py:704
  154.9 1.3 copy.11

commit v8 on v7

--- a/solution.py
+++ b/solution.py
@@ -247,7 +247,7 @@
     eps_ref, mass_hbm, q_hbm, src_hbm, tgt_hbm, plan_hbm, fsrc_hbm, ftgt_hbm, out_ref,
     stage_ref, stage2_ref, feat_ref, plan_ref, tgt_ref, src_ref, fsrc_ref, ftgt_ref, a_ref, cross_ref, cost_ref, kern_ref,
     early_ref, p_ref, q_ref, u_ref, v_ref, dots_ref, other_ref, part_ref, gath_ref, msg_ref, news_ref, mass_ref, mass2_ref,
-    load_sem, plan_send, plan_recv, tgt_send, tgt_recv, feat_send, feat_recv, sum_send, sum_recv, a_send, a_recv,
+    load_sem, plan_send, plan_recv, tgt_send, tgt_recv, feat_send, feat_recv, sum_send, sum_recv,
     swap_send, swap_recv, early_send, early_recv, msg_send, msg_recv,
 ):
     at = Place()
@@ -343,7 +343,11 @@
         device_id={"rows": at.sib})
     swap_feat.start()
     load_src.wait()
-    src_ref[...] = cost_ref[:rows, :].astype(jnp.bfloat16)
+    src_ref[:rows] = cost_ref[:rows, :].astype(jnp.bfloat16)
+    swap_src = pltpu.make_async_remote_copy(
+        src_ref=src_ref.at[:rows], dst_ref=src_ref.at[rows:], send_sem=swap_send.at[2], recv_sem=swap_recv.at[2],
+        device_id={"rows": at.sib})
+    swap_src.start()
     eye = lax.broadcasted_iota(jnp.int32, (LANES, LANES), 0) == lax.broadcasted_iota(jnp.int32, (LANES, LANES), 1)
     swap.wait()
     for r in range(rows // LANES):
@@ -359,17 +363,7 @@
         def _():
             f(rows)
 
-    def a_copy(j):
-        cols_at = pl.ds(pl.multiple_of(j * BLK, BLK), BLK)
-        return pltpu.make_async_remote_copy(
-            src_ref=a_ref.at[:rows, cols_at], dst_ref=a_ref.at[rows:, cols_at], send_sem=a_send.at[j],
-            recv_sem=a_recv.at[j], device_id={"rows": at.sib})
-
     def add_column(j):
-        @pl.when(at.core == 1)
-        def _():
-            a_copy(j).wait_recv()
-
         def add(reach, base_ref):
             lhs = a_ref[:reach, pl.ds(pl.multiple_of(j * BLK, BLK), BLK)]
             for col in range(nblk):
@@ -389,16 +383,12 @@
         on_reach(go)
 
     def column(j):
-        prod = jnp.dot(src_ref[...], plan_ref[j], preferred_element_type=jnp.float32)
-        a_ref[:rows, pl.ds(pl.multiple_of(j * BLK, BLK), BLK)] = prod.astype(jnp.bfloat16)
-
-        @pl.when(at.core == 0)
-        def _():
-            a_copy(j).start()
-
-        @pl.when(j > 0)
-        def _():
-            add_column(j - 1)
+        def go(reach):
+            prod = jnp.dot(src_ref[:reach, :], plan_ref[j], preferred_element_type=jnp.float32)
+            a_ref[:reach, pl.ds(pl.multiple_of(j * BLK, BLK), BLK)] = prod.astype(jnp.bfloat16)
+
+        on_reach(go)
+        add_column(j)
 
     def cast_plan(j):
         load_plan(j).wait()
@@ -505,6 +495,7 @@
     for owner in (at.sib, at.x1, at.y1, at.d1):
         fcopy(owner, at.sib, 0).wait_recv()
     swap_feat.wait()
+    swap_src.wait()
 
     def crosses(reach):
         def cross(j, carry):
@@ -526,7 +517,6 @@
     mirror(at.d0 - at.core, at.d0 - at.core + 1)
 
     go_on()
-    add_column(nblk - 1)
 
     for kind in range(7):
         fcopy(me, at.sib, kind).wait_send()
@@ -555,17 +545,6 @@
 
     lax.fori_loop(0, nblk, sib_done, 0)
 
-    def a_done():
-        @pl.when(at.core == 0)
-        def _():
-            def body(j, carry):
-                a_copy(j).wait_send()
-                return carry
-
-            lax.fori_loop(0, nblk, body, 0)
-
-    a_done()
-
     def early(src, j, slot, dest, kind):
         return pltpu.make_async_remote_copy(
             src_ref=src, dst_ref=early_ref.at[slot, j], send_sem=early_send.at[kind, j],
@@ -656,8 +635,6 @@
                 msg_ref[tiles + r:tiles + r + 1] = jnp.sum(jnp.where(eye, scale, 0.0), axis=0, keepdims=True)
             for k in range(reach):
                 news(k).start()
-            for k in range(reach):
-                news(k).wait_send()
 
         @pl.when(at.core == 0)
         def _():
@@ -671,6 +648,12 @@
                 for k in range(1, reach):
                     other_ref[k - 1, r * LANES:(r + 1) * LANES, :] = spread(news_ref[k, tiles + r:tiles + r + 1], eye)
 
+    def news_done(reach):
+        @pl.when(at.core == 1)
+        def _():
+            for k in range(reach):
+                news(k).wait_send()
+
     def own_block(j):
         cols_at = pl.multiple_of(j * BLK, BLK)
         return plan_block(lambda h: kern_ref[0, :, pl.ds(cols_at + h * LANES, LANES)], u_ref[:rows, :], v_ref, j)
@@ -686,12 +669,12 @@
     begin, go_on = gather_plan(at, nblk, plan_ref, plan_send, plan_recv, next_plan, column, form)
     begin()
     go_on()
-    add_column(nblk - 1)
-    a_done()
+    news_done(len(across))
     sweeps(False)
 
     for j in range(nblk):
         out_ref[:, j * BLK:(j + 1) * BLK] = own_block(j)
+    news_done(1)
 
 
 def fgw(src, tgt, plan, mass, q, fsrc, ftgt, eps):
@@ -712,7 +695,7 @@
             pltpu.VMEM((2, BLK, BLK), f32),
             pltpu.VMEM((nblk, DEV * BLK, BLK), bf16),
             pltpu.VMEM((nblk, DEV * BLK, BLK), bf16),
-            pltpu.VMEM((rows, cols), bf16),
+            pltpu.VMEM((2 * rows, cols), bf16),
             pltpu.VMEM((2 * BLK, BLK), bf16),
             pltpu.VMEM((DEV * BLK, BLK), bf16),
             pltpu.VMEM((2 * rows, cols), bf16),
@@ -741,10 +724,8 @@
             pltpu.SemaphoreType.DMA((DEV,)),
             pltpu.SemaphoreType.DMA((2, PIECES, 3)),
             pltpu.SemaphoreType.DMA((2, PIECES, DEV // 2)),
-            pltpu.SemaphoreType.DMA((nblk,)),
-            pltpu.SemaphoreType.DMA((nblk,)),
-            pltpu.SemaphoreType.DMA((2,)),
-            pltpu.SemaphoreType.DMA((2,)),
+            pltpu.SemaphoreType.DMA((3,)),
+            pltpu.SemaphoreType.DMA((3,)),
             pltpu.SemaphoreType.DMA((3, EARLY + 1)),
             pltpu.SemaphoreType.DMA((3, EARLY + 1)),
             pltpu.SemaphoreType.DMA((4,)),

time: 156 us -> 156 us (level)
  no operation moved by 1% of the time
where the time goes in v8:
time: 156 us
  Pallas kernels  154 us (99%)
    pallas_call x1, Pallas kernels, fgw(): pl.pallas_call(fgw_kernel, out_shape=jax.ShapeDtypeStruct((rows, cols), f...  154 us

profile of v8, /device:TPU:0, one launch (start us, length us, event | category | flops | bytes accessed | tf_op | source)
XLA Modules:
  0.0 155.7 jit_solution(408088955750539230)
XLA Ops:
  0.7 153.7 %fgw.1 = f32[256,2048]{1,0:T(8,128)S(1)} custom-call(f32[1]{0:T(128)} %bitcast.3.eps_ref, f32[2,128]{1,0:T(2,128)} %bitcast.5, f32[16,128]{1,0:T(8,128)} %bitcast.4, f32[256,2048]{1,0:T(8,128)} %src_hbm.1, f32[256,2048]{1,0:T(8,128)} %tgt_hbm.1, f32[256,2048]{1,0:T(8,128)} %plan_hbm.1, f32[256,256]{1,0:T(8,128)} %fsrc_hbm.1, f32[256,256]{1,0:T(8,128)} %ftgt_hbm.1), custom_call_target="tpu_custom_call" | custom-call | tf_op jit(solution)/shard_map/fgw/pallas_call | solution.py:687
  154.4 1.3 copy.11

commit v9 on v8

--- a/solution.py
+++ b/solution.py
@@ -58,7 +58,7 @@
             kern_ref[half, pl.ds(row, SUB), t * LANES:(t + 1) * LANES] = jnp.exp((low - vals[t]) * inv_eps)
         return carry
 
-    lax.fori_loop(0, rows // SUB, block, 0, unroll=8)
+    lax.fori_loop(0, rows // SUB, block, 0, unroll=16)
 
 
 def spread(line, eye):

time: 156 us -> 155 us (level)
  no operation moved by 1% of the time
where the time goes in v9:
time: 155 us
  Pallas kernels  153 us (99%)
    pallas_call x1, Pallas kernels, fgw(): pl.pallas_call(fgw_kernel, out_shape=jax.ShapeDtypeStruct((rows, cols), f...  153 us

profile of v9, /device:TPU:0, one launch (start us, length us, event | category | flops | bytes accessed | tf_op | source)
XLA Modules:
  0.0 155.1 jit_solution(2829776470118523477)
XLA Ops:
  0.7 153.1 %fgw.1 = f32[256,2048]{1,0:T(8,128)S(1)} custom-call(f32[1]{0:T(128)} %bitcast.3.eps_ref, f32[2,128]{1,0:T(2,128)} %bitcast.5, f32[16,128]{1,0:T(8,128)} %bitcast.4, f32[256,2048]{1,0:T(8,128)} %src_hbm.1, f32[256,2048]{1,0:T(8,128)} %tgt_hbm.1, f32[256,2048]{1,0:T(8,128)} %plan_hbm.1, f32[256,256]{1,0:T(8,128)} %fsrc_hbm.1, f32[256,256]{1,0:T(8,128)} %ftgt_hbm.1), custom_call_target="tpu_custom_call" | custom-call | tf_op jit(solution)/shard_map/fgw/pallas_call | solution.py:687
  153.8 1.3 copy.11

commit v10 on v9

--- a/solution.py
+++ b/solution.py
@@ -50,7 +50,7 @@
 
     def block(b, carry):
         row = pl.multiple_of(b * SUB, SUB)
-        at_row = pl.ds(half * rows + row, SUB)
+        at_row = pl.ds(pl.multiple_of(half * rows + row, SUB), SUB)
         vals = [cost_ref[at_row, t * LANES:(t + 1) * LANES] for t in range(tiles)]
         low = functools.reduce(jnp.minimum, vals)
         low = jnp.min(low, axis=1, keepdims=True)
@@ -622,11 +622,14 @@
 
     def sweeps(first):
         reach = len(across) if first else 1
-        build_kernel(cost_ref, kern_ref, eps, 0, rows, cols)
+        def build(half, carry):
+            build_kernel(cost_ref, kern_ref, eps, half, rows, cols)
+            return carry
+
+        lax.fori_loop(0, 1 + at.core, build, 0)
 
         @pl.when(at.core == 1)
         def _():
-            build_kernel(cost_ref, kern_ref, eps, 1, rows, cols)
             sinkhorn(at, kern_ref, p_ref, q_ref, u_ref, v_ref, dots_ref, part_ref, gath_ref, sum_send, sum_recv)
             msg_ref[:tiles] = v_ref[...]
             msg_ref[tiles:] = jnp.zeros_like(msg_ref[tiles:])

time: 155 us -> 155 us (level)
  no operation moved by 1% of the time
where the time goes in v10:
time: 155 us
  Pallas kernels  153 us (99%)
    pallas_call x1, Pallas kernels, fgw(): pl.pallas_call(fgw_kernel, out_shape=jax.ShapeDtypeStruct((rows, cols), f...  153 us

profile of v10, /device:TPU:0, one launch (start us, length us, event | category | flops | bytes accessed | tf_op | source)
XLA Modules:
  0.0 155.1 jit_solution(9365222655634457090)
XLA Ops:
  0.7 153.2 %fgw.1 = f32[256,2048]{1,0:T(8,128)S(1)} custom-call(f32[1]{0:T(128)} %bitcast.3.eps_ref, f32[2,128]{1,0:T(2,128)} %bitcast.5, f32[16,128]{1,0:T(8,128)} %bitcast.4, f32[256,2048]{1,0:T(8,128)} %src_hbm.1, f32[256,2048]{1,0:T(8,128)} %tgt_hbm.1, f32[256,2048]{1,0:T(8,128)} %plan_hbm.1, f32[256,256]{1,0:T(8,128)} %fsrc_hbm.1, f32[256,256]{1,0:T(8,128)} %ftgt_hbm.1), custom_call_target="tpu_custom_call" | custom-call | tf_op jit(solution)/shard_map/fgw/pallas_call | solution.py:690
  153.8 1.3 copy.11
